TPU v7x, 512 devices: a whole 4x8x8 slice. The times are simulated.
512 devices in a mesh: seq: 64 (over x, z, core), res: 8 (over y).
Axes of the slice: x: 4, y: 8, z: 8, core: 2. Of those that a mesh axis runs over, the one named last changes fastest.
Arguments:
- alignment_rows: bfloat16 [4096, 64, 64], P('seq', 'res'), may hold values from -6 to 6
- pair_features: bfloat16 [64, 64, 128], P('res', 'seq'), may hold values from -6 to 6
- sequence_block_count: int32 [64], P('seq'), may hold values from 16 to 64
- cluster_member_count: int32 [4096], P('seq'), may hold values from 1 to 16
- residue_present_mask: int32 [64], replicated, may hold values 0 or 1
- attention_in_weight: bfloat16 [64, 256], replicated, may hold values from -0.75 to 0.75
- attention_out_weight: bfloat16 [64, 64], replicated, may hold values from -4 to 4
- pair_bias_weight: float32 [128, 8], replicated, may hold values from -48 to 48
- outer_factor_weight: bfloat16 [64, 64], replicated, may hold values from -0.75 to 0.75
- outer_output_weight: float32 [1024, 128], replicated, may hold values from -4 to 4
- outer_product_bias: float32 [128], replicated, may hold values from -3 to 3
Outputs:
- row_attention_update: bfloat16 [4096, 64, 64], P('seq', 'res')
- pair_update: bfloat16 [64, 64, 128], P('seq', 'res')
All inputs are finite; a program needn't handle non-finite values.
Results may differ from a plain program's by a relative error of at most 0.0081.
Values may be sent and summed in bfloat16 or wider, within the bound.
No kernel may reach another device: no remote copies, remote signals or barrier semaphores. Data moves between devices by JAX's collectives and lax.ppermute only.
A program may use at most 64 MiB of HBM per device.

v0:
```python
import math

import jax
import jax.numpy as jnp
from jax import lax
from jax.sharding import PartitionSpec as P


def from_everyone(shard, axis):
    copies = jnp.broadcast_to(shard, (lax.axis_size(axis), *shard.shape))
    return lax.all_to_all(copies, axis, split_axis=0, concat_axis=0, tiled=True)


def over_copies(shard, axis):
    everything = from_everyone(shard, axis)
    return jnp.sum(everything, axis=0)


def in_order(pieces, dim):
    pieces = jnp.moveaxis(pieces, 0, dim)
    lengths = pieces.shape
    return pieces.reshape(*lengths[:dim], lengths[dim] * lengths[dim + 1], *lengths[dim + 2 :])


def collect(shard, axis, dim):
    pieces = from_everyone(shard, axis)
    return in_order(pieces, dim)


def cut_along(shard, dim, devices):
    lengths = shard.shape
    pieces = shard.reshape(*lengths[:dim], devices, lengths[dim] // devices, *lengths[dim + 1 :])
    return jnp.moveaxis(pieces, dim, 0)


def summed_on_arrival(shard, axis, dim):
    pieces = cut_along(shard, dim, lax.axis_size(axis))
    arrived = lax.all_to_all(pieces, axis, split_axis=0, concat_axis=0, tiled=True)
    return arrived.astype(jnp.float32).sum(axis=0)


def apply_layer_norm(values):
    centre = jnp.mean(values, axis=-1, keepdims=True)
    spread = jnp.mean(jnp.square(values - centre), axis=-1, keepdims=True)
    return (values - centre) * lax.rsqrt(spread + 1e-05)


def apply_row_projection(input_rows, attention_in_weight):
    slot_count, n_res, channel_width = input_rows.shape
    normed_alignment = apply_layer_norm(input_rows.astype(jnp.float32)).astype(jnp.bfloat16)
    projected_rows = jnp.dot(
        normed_alignment.reshape(-1, channel_width),
        attention_in_weight,
        preferred_element_type=jnp.float32,
    ).reshape(slot_count, n_res, 4 * channel_width)
    return projected_rows


def split_projection_parts(projected_rows, head_count):
    channel_width = projected_rows.shape[-1] // 4
    head_dim = channel_width // head_count
    query_rows = (projected_rows[..., :channel_width] * (1.0 / math.sqrt(head_dim))).astype(
        jnp.bfloat16
    )
    key_value_pairs = projected_rows[..., channel_width : 3 * channel_width].astype(jnp.bfloat16)
    gate_activation = jax.nn.sigmoid(projected_rows[..., 3 * channel_width :])
    return (query_rows, key_value_pairs, gate_activation)


def attend(query_rows, key_value_pairs, gate_activation, full_bias, attention_out_weight):
    slot_count, n_query, channel_width = query_rows.shape
    head_count = full_bias.shape[0]
    head_dim = channel_width // head_count
    n_keys = key_value_pairs.shape[1]
    block = math.gcd(slot_count, max(1, (1 << 18) // (head_count * n_query * n_keys)))

    def one_block(pieces):
        query_blk, kv_blk = pieces
        query_heads = query_blk.reshape(block, n_query, head_count, head_dim)
        key_heads = kv_blk[..., :channel_width].reshape(block, n_keys, head_count, head_dim)
        value_heads = kv_blk[..., channel_width:].reshape(block, n_keys, head_count, head_dim)
        scores = (
            jnp.einsum(
                "bihd,bjhd->bhij", query_heads, key_heads, preferred_element_type=jnp.float32
            )
            + full_bias[None]
        )
        row_max = jnp.max(scores, axis=-1, keepdims=True)
        expo = jnp.exp(scores - row_max)
        probs = (expo / jnp.sum(expo, axis=-1, keepdims=True)).astype(jnp.bfloat16)
        context = jnp.einsum(
            "bhij,bjhd->bihd", probs, value_heads, preferred_element_type=jnp.float32
        )
        return context.reshape(block, n_query, channel_width)

    context = lax.map(
        one_block,
        (
            query_rows.reshape(-1, block, n_query, channel_width),
            key_value_pairs.reshape(-1, block, n_keys, 2 * channel_width),
        ),
    )
    context = context.reshape(slot_count, n_query, channel_width)
    gated = (gate_activation * context).astype(jnp.bfloat16)
    update = jnp.dot(
        gated.reshape(-1, channel_width), attention_out_weight, preferred_element_type=jnp.float32
    ).astype(jnp.bfloat16)
    return update.reshape(slot_count, n_query, channel_width)


def local(
    alignment_rows,
    pair_features,
    sequence_block_count,
    cluster_member_count,
    residue_present_mask,
    attention_in_weight,
    attention_out_weight,
    pair_bias_weight,
    outer_factor_weight,
    outer_output_weight,
    outer_product_bias,
):
    slot_count, local_residues, channel_width = alignment_rows.shape
    head_count = pair_bias_weight.shape[1]
    block_length = local_residues * lax.axis_size("res")
    factor_width = outer_factor_weight.shape[1] // 2
    pair_width = outer_output_weight.shape[1]
    usable = (jnp.arange(slot_count, dtype=jnp.int32) < sequence_block_count[0]).astype(jnp.float32)
    seq_weight = cluster_member_count.astype(jnp.float32) * usable
    weight_sum = over_copies(jnp.sum(seq_weight), "seq")
    key_mask = jnp.where(residue_present_mask == 1, 0.0, -1000000.0).astype(jnp.float32)
    pair_norm = apply_layer_norm(pair_features.astype(jnp.float32))
    bias_tile = jnp.einsum(
        "ijp,ph->hij", pair_norm, pair_bias_weight, precision=lax.Precision.HIGHEST
    )
    bias_local = collect(bias_tile, "seq", 2) + key_mask[None, None, :]
    flat_rows = alignment_rows.reshape(slot_count, local_residues * channel_width)
    arrived = lax.all_to_all(flat_rows, "res", split_axis=0, concat_axis=1, tiled=True).reshape(
        -1, block_length, channel_width
    )
    full_bias = collect(bias_local, "res", 1)
    query_rows, key_value_pairs, gate_activation = split_projection_parts(
        apply_row_projection(arrived, attention_in_weight), head_count
    )
    update = attend(query_rows, key_value_pairs, gate_activation, full_bias, attention_out_weight)
    returned = lax.all_to_all(
        update.reshape(-1, block_length * channel_width),
        "res",
        split_axis=1,
        concat_axis=0,
        tiled=True,
    )
    returned = returned.reshape(slot_count, local_residues, channel_width)
    row_attention_update = returned * usable.astype(jnp.bfloat16)[:, None, None]
    updated_alignment = alignment_rows.astype(jnp.float32) + row_attention_update.astype(
        jnp.float32
    )
    outer_input_norm = apply_layer_norm(updated_alignment).astype(jnp.bfloat16)
    factors = jnp.dot(
        outer_input_norm.reshape(-1, channel_width),
        outer_factor_weight,
        preferred_element_type=jnp.float32,
    ).reshape(slot_count, local_residues, 2 * factor_width)
    res_start = lax.axis_index("res") * local_residues
    res_keep = lax.dynamic_slice_in_dim(residue_present_mask, res_start, local_residues).astype(
        jnp.float32
    )[None, :, None]
    left_proj = (factors[..., :factor_width] * res_keep).astype(jnp.bfloat16)
    right_proj = (factors[..., factor_width:] * res_keep * seq_weight[:, None, None]).astype(
        jnp.bfloat16
    )
    left_all = collect(left_proj.reshape(slot_count, local_residues * factor_width), "res", 1)
    left_all = left_all.reshape(slot_count, block_length, factor_width)
    right_flat = right_proj.reshape(slot_count, local_residues * factor_width)
    weight_cube = outer_output_weight.reshape(factor_width, factor_width, pair_width)
    block = math.gcd(block_length // lax.axis_size("seq") * lax.axis_size("seq"), 16)

    def block_term(block_index):
        left_block = lax.dynamic_slice_in_dim(left_all, block_index * block, block, 1)
        outer_block = lax.dot_general(
            left_block.reshape(slot_count, block * factor_width),
            right_flat,
            (((0,), (0,)), ((), ())),
            preferred_element_type=jnp.float32,
        )
        outer_block = outer_block.reshape(block, factor_width, local_residues, factor_width)
        return jnp.einsum(
            "icjd,cdp->ijp", outer_block, weight_cube, precision=lax.Precision.HIGHEST
        )

    blocks_out = lax.map(
        block_term,
        jnp.arange(
            block_length // lax.axis_size("seq") * lax.axis_size("seq") // block, dtype=jnp.int32
        ),
    )
    summed = summed_on_arrival(
        blocks_out.reshape(
            block_length // lax.axis_size("seq") * lax.axis_size("seq"), local_residues, pair_width
        ).astype(jnp.bfloat16),
        "seq",
        0,
    )
    pair_update = (summed / weight_sum + outer_product_bias).astype(jnp.bfloat16)
    return (row_attention_update, pair_update)


def solution(mesh):
    return jax.shard_map(
        local,
        mesh=mesh,
        in_specs=(
            P("seq", "res", None),
            P("res", "seq", None),
            P("seq"),
            P("seq"),
            P(),
            P(),
            P(),
            P(),
            P(),
            P(),
            P(),
        ),
        out_specs=(P("seq", "res", None), P("seq", "res", None)),
        check_vma=False,
    )
```

profile of v0, /device:TPU:1, one launch (start us, length us, event | category | flops | bytes accessed | tf_op | source)
XLA Modules:
  0.0 144.2 jit_solution(6712411401909029182)
XLA Ops:
  0.6 0.8 convert_reduce_fusion.1
  1.5 0.9 fusion.48
  2.3 0.9 convolution_bitcast_fusion.1
  3.3 0.7 broadcast_in_dim.46
  4.0 14.8 %all-to-all-start.1 = ((f32[64,8,8,1]{2,1,3,0:T(8,128)}), f32[64,8,8,1]{2,1,3,0:T(8,128)S(1)}, u32[]{:S(2)}, u32[]{:S(2)}) async-start(f32[64,8,8,1]{2,1,3,0:T(8,128)} %broadcast_in_dim.46), calls=%async_computation.1 | async-start | bytes 524288 | tf_op jit(solution)/shard_map/all_to_all | solution.py:11
  18.9 0.7 compare_select_fusion
  20.2 1.3 fusion.55
  21.4 1.7 %all_to_all.38 = bf16[8,8,512]{2,1,0:T(8,128)(2,1)} reshape(bf16[64,8,64]{2,1,0:T(8,128)(2,1)} %param.13) | data formatting | bytes 131072 | tf_op jit(solution)/shard_map/all_to_all | solution.py:139
  23.1 7.7 %all-to-all-done.1 = f32[64,8,8,1]{2,1,3,0:T(8,128)S(1)} async-done(((f32[64,8,8,1]{2,1,3,0:T(8,128)}), f32[64,8,8,1]{2,1,3,0:T(8,128)S(1)}, u32[]{:S(2)}, u32[]{:S(2)}) %all-to-all-start.1) | async-done | bytes 16416 | tf_op jit(solution)/shard_map/all_to_all | solution.py:11
  30.8 6.8 %all-to-all-start = ((bf16[8,8,512]{2,1,0:T(8,128)(2,1)}), bf16[8,8,512]{2,1,0:T(8,128)(2,1)S(1)}, u32[]{:S(2)}, u32[]{:S(2)}) async-start(bf16[8,8,512]{2,1,0:T(8,128)(2,1)} %all_to_all.38), calls=%async_computation | async-start | bytes 131072 | tf_op jit(solution)/shard_map/all_to_all | solution.py:139
  37.9 0.8 reshape.231
  38.8 6.1 %all-to-all-done = bf16[8,8,512]{2,1,0:T(8,128)(2,1)S(1)} async-done(((bf16[8,8,512]{2,1,0:T(8,128)(2,1)}), bf16[8,8,512]{2,1,0:T(8,128)(2,1)S(1)}, u32[]{:S(2)}, u32[]{:S(2)}) %all-to-all-start) | async-done | bytes 65568 | tf_op jit(solution)/shard_map/all_to_all | solution.py:139
  44.9 3.4 %all-to-all-start.2 = ((f32[8,1,4096]{2,1,0:T(1,128)}), f32[8,1,4096]{2,1,0:T(1,128)S(1)}, u32[]{:S(2)}, u32[]{:S(2)}) async-start(f32[8,1,4096]{2,1,0:T(1,128)} %reshape.231), calls=%async_computation.2 | async-start | bytes 262144 | tf_op jit(solution)/shard_map/all_to_all | solution.py:11
  48.6 0.3 multiply_reduce_fusion.1
  48.9 0.3 fusion.57
  49.8 6.3 %all-to-all-done.2 = f32[8,1,4096]{2,1,0:T(1,128)S(1)} async-done(((f32[8,1,4096]{2,1,0:T(1,128)}), f32[8,1,4096]{2,1,0:T(1,128)S(1)}, u32[]{:S(2)}, u32[]{:S(2)}) %all-to-all-start.2) | async-done | bytes 131104 | tf_op jit(solution)/shard_map/all_to_all | solution.py:11
  56.1 0.5 broadcast.134
  56.7 1.0 reduce.4
  57.9 2.3 %fusion.58 = (f32[8,8,64]{2,1,0:T(8,128)S(1)}, f32[8,8,64,64]{2,3,1,0:T(8,128)}) fusion(f32[8,64,64]{1,2,0:T(8,128)S(1)} %copy.90, bf16[8,64,64]{1,2,0:T(8,128)(2,1)S(1)} %copy.86, bf16[8,64,64]{1,2,0:T(8,128)(2,1)S(1)} %copy.85), kind=kOutput, calls=%fused_computation.81 | convolution fusion | flops 4980799 | bytes 1327104 | tf_op jit(solution)/shard_map/while/body/eval_jaxpr/sub | solution.py:89
  60.2 2.0 %convolution_bitcast_fusion = f32[8,64,64]{1,2,0:T(8,128)S(1)} fusion(f32[8,8,64,64]{2,3,1,0:T(8,128)} %get-tuple-element.79, f32[8,8,64]{2,1,0:T(8,128)S(1)} %get-tuple-element.78, bf16[8,64,64]{1,2,0:T(8,128)(2,1)S(1)} %copy.84), kind=kOutput, calls=%fused_computation.14 | convolution fusion | flops 4718592 | bytes 1261568 | tf_op jit(solution)/shard_map/while/body/eval_jaxpr/bhij,bjhd->bihd/dot_general | solution.py:91
  63.0 0.7 copy.94
  63.6 3.4 %all-to-all-start.3 = ((bf16[8,8,512]{2,0,1:T(8,128)(2,1)}), bf16[8,8,512]{2,0,1:T(8,128)(2,1)S(1)}, u32[]{:S(2)}, u32[]{:S(2)}) async-start(bf16[8,8,512]{2,0,1:T(8,128)(2,1)} %copy.94), calls=%async_computation.3 | async-start | bytes 131072 | tf_op jit(solution)/shard_map/all_to_all | solution.py:147
  67.1 7.0 %all-to-all-done.3 = bf16[8,8,512]{2,0,1:T(8,128)(2,1)S(1)} async-done(((bf16[8,8,512]{2,0,1:T(8,128)(2,1)}), bf16[8,8,512]{2,0,1:T(8,128)(2,1)S(1)}, u32[]{:S(2)}, u32[]{:S(2)}) %all-to-all-start.3) | async-done | bytes 65568 | tf_op jit(solution)/shard_map/all_to_all | solution.py:147
  74.3 0.2 fusion.23
  75.0 0.3 fusion.40
  75.5 0.7 broadcast_in_dim.51
  76.2 3.4 %all-to-all-start.4 = ((bf16[8,64,256]{2,1,0:T(8,128)(2,1)}), bf16[8,64,256]{2,1,0:T(8,128)(2,1)S(1)}, u32[]{:S(2)}, u32[]{:S(2)}) async-start(bf16[8,64,256]{2,1,0:T(8,128)(2,1)} %broadcast_in_dim.51), calls=%async_computation.4 | async-start | bytes 524288 | tf_op jit(solution)/shard_map/all_to_all | solution.py:11
  79.6 9.2 %all-to-all-done.4 = bf16[8,64,256]{2,1,0:T(8,128)(2,1)S(1)} async-done(((bf16[8,64,256]{2,1,0:T(8,128)(2,1)}), bf16[8,64,256]{2,1,0:T(8,128)(2,1)S(1)}, u32[]{:S(2)}, u32[]{:S(2)}) %all-to-all-start.4) | async-done | bytes 262176 | tf_op jit(solution)/shard_map/all_to_all | solution.py:11
  88.9 1.2 broadcast_in_dim.52
  90.1 10.9 %all-to-all-start.6 = ((f32[64,1,1]{2,1,0:T(1,128)}), f32[64,1,1]{2,1,0:T(1,128)S(1)}, u32[]{:S(2)}, u32[]{:S(2)}) async-start(f32[64,1,1]{2,1,0:T(1,128)} %broadcast_in_dim.52), calls=%async_computation.6 | async-start | bytes 65536 | tf_op jit(solution)/shard_map/all_to_all | solution.py:11
  101.0 0.3 copy.98
  101.3 20.8 %while.2 = (s32[]{:T(128)}, bf16[4,16,8,128]{3,2,1,0:T(8,128)(2,1)}, s32[4]{0:T(128)S(1)}, bf16[64,64,32]{0,2,1:T(8,128)(2,1)S(1)}, bf16[64,256]{0,1:T(8,128)(2,...) while((s32[]{:T(128)}, bf16[4,16,8,128]{3,2,1,0:T(8,128)(2,1)}, ...), condition=%wide.region_9.10_spmd, body=%wide.region_8.9_spmd.sunk | while | flops 218103808 | bytes 1835683 | solution.py:192
  101.3 0.6 dynamic_slice.25
  102.6 0.4 fusion.77
  103.0 3.5 %fusion.78 = bf16[4,16,8,128]{3,2,1,0:T(8,128)(2,1)} fusion(bf16[4,16,8,128]{3,2,1,0:T(8,128)(2,1)} %get-tuple-element.128, s32[]{:T(128)} %get-tuple-element.127, f32[16,32,8,32]{3,1,2,0:T(8,128)S(1)} %fusion.77, f32[32,32,128]{2,1,0:T(8,128)S(1)} %get-tuple-element.142), kind=kOutput, calls=%fused_computation.3.clone.1 | convolution fusion | flops 201326592 | bytes 1114624 | tf_op jit(solution)/shard_map/while/body/eval_jaxpr/icjd,cdp->ijp/dot_general | solution.py:188
  106.5 0.6 dynamic_slice.25
  107.8 0.5 fusion.77
  108.2 3.5 %fusion.78 = bf16[4,16,8,128]{3,2,1,0:T(8,128)(2,1)} fusion(bf16[4,16,8,128]{3,2,1,0:T(8,128)(2,1)} %get-tuple-element.128, s32[]{:T(128)} %get-tuple-element.127, f32[16,32,8,32]{3,1,2,0:T(8,128)S(1)} %fusion.77, f32[32,32,128]{2,1,0:T(8,128)S(1)} %get-tuple-element.142), kind=kOutput, calls=%fused_computation.3.clone.1 | convolution fusion | flops 201326592 | bytes 1114624 | tf_op jit(solution)/shard_map/while/body/eval_jaxpr/icjd,cdp->ijp/dot_general | solution.py:188
  111.7 0.6 dynamic_slice.25
  113.0 0.5 fusion.77
  113.4 3.5 %fusion.78 = bf16[4,16,8,128]{3,2,1,0:T(8,128)(2,1)} fusion(bf16[4,16,8,128]{3,2,1,0:T(8,128)(2,1)} %get-tuple-element.128, s32[]{:T(128)} %get-tuple-element.127, f32[16,32,8,32]{3,1,2,0:T(8,128)S(1)} %fusion.77, f32[32,32,128]{2,1,0:T(8,128)S(1)} %get-tuple-element.142), kind=kOutput, calls=%fused_computation.3.clone.1 | convolution fusion | flops 201326592 | bytes 1114624 | tf_op jit(solution)/shard_map/while/body/eval_jaxpr/icjd,cdp->ijp/dot_general | solution.py:188
  116.9 0.6 dynamic_slice.25
  118.2 0.5 fusion.77
  118.6 3.5 %fusion.78 = bf16[4,16,8,128]{3,2,1,0:T(8,128)(2,1)} fusion(bf16[4,16,8,128]{3,2,1,0:T(8,128)(2,1)} %get-tuple-element.128, s32[]{:T(128)} %get-tuple-element.127, f32[16,32,8,32]{3,1,2,0:T(8,128)S(1)} %fusion.77, f32[32,32,128]{2,1,0:T(8,128)S(1)} %get-tuple-element.142), kind=kOutput, calls=%fused_computation.3.clone.1 | convolution fusion | flops 201326592 | bytes 1114624 | tf_op jit(solution)/shard_map/while/body/eval_jaxpr/icjd,cdp->ijp/dot_general | solution.py:188
  122.1 10.3 %all-to-all-start.5 = ((bf16[64,1,8,128]{3,2,1,0:T(8,128)(2,1)}), bf16[64,1,8,128]{3,2,1,0:T(8,128)(2,1)S(1)}, u32[]{:S(2)}, u32[]{:S(2)}) async-start(bf16[64,1,8,128]{3,2,1,0:T(8,128)(2,1)} %bitcast.35), calls=%async_computation.5 | async-start | bytes 262144 | tf_op jit(solution)/shard_map/all_to_all | solution.py:38
  132.5 0.7 reduce_sum.100
  133.2 9.6 %all-to-all-done.5 = bf16[64,1,8,128]{3,2,1,0:T(8,128)(2,1)S(1)} async-done(((bf16[64,1,8,128]{3,2,1,0:T(8,128)(2,1)}), bf16[64,1,8,128]{3,2,1,0:T(8,128)(2,1)S(1)}, u32[]{:S(2)}, u32[]{:S(2)}) %all-to-all-start.5) | async-done | bytes 131104 | tf_op jit(solution)/shard_map/all_to_all | solution.py:38
  142.9 1.3 fusion.51
  (54 shorter events, 3.2 us)
Async XLA Ops:
  0.6 48.3 %copy-start = (bf16[64,256]{1,0:T(8,128)(2,1)S(1)}, bf16[64,256]{1,0:T(8,128)(2,1)}, u32[]{:S(2)}) copy-start(bf16[64,256]{1,0:T(8,128)(2,1)} %param.18) | copy-start | bytes 98308
  4.0 26.8 %all-to-all-start.1 = ((f32[64,8,8,1]{2,1,3,0:T(8,128)}), f32[64,8,8,1]{2,1,3,0:T(8,128)S(1)}, u32[]{:S(2)}, u32[]{:S(2)}) async-start(f32[64,8,8,1]{2,1,3,0:T(8,128)} %broadcast_in_dim.46), calls=%async_computation.1 | async-start | bytes 524288 | tf_op jit(solution)/shard_map/all_to_all | solution.py:11
  30.8 14.1 %all-to-all-start = ((bf16[8,8,512]{2,1,0:T(8,128)(2,1)}), bf16[8,8,512]{2,1,0:T(8,128)(2,1)S(1)}, u32[]{:S(2)}, u32[]{:S(2)}) async-start(bf16[8,8,512]{2,1,0:T(8,128)(2,1)} %all_to_all.38), calls=%async_computation | async-start | bytes 131072 | tf_op jit(solution)/shard_map/all_to_all | solution.py:139
  44.9 11.3 %all-to-all-start.2 = ((f32[8,1,4096]{2,1,0:T(1,128)}), f32[8,1,4096]{2,1,0:T(1,128)S(1)}, u32[]{:S(2)}, u32[]{:S(2)}) async-start(f32[8,1,4096]{2,1,0:T(1,128)} %reshape.231), calls=%async_computation.2 | async-start | bytes 262144 | tf_op jit(solution)/shard_map/all_to_all | solution.py:11
  60.1 2.3 %copy-start.5 = (bf16[64,64]{1,0:T(8,128)(2,1)S(1)}, bf16[64,64]{1,0:T(8,128)(2,1)}, u32[]{:S(2)}) copy-start(bf16[64,64]{1,0:T(8,128)(2,1)} %param.19) | copy-start | bytes 24580
  60.2 6.9 %copy-start.7 = (s32[64]{0:T(128)S(1)}, s32[64]{0:T(128)}, u32[]{:S(2)}) copy-start(s32[64]{0:T(128)} %param.17) | copy-start | bytes 772
  62.2 12.1 %copy-start.2 = (bf16[64,8,64]{2,1,0:T(8,128)(2,1)S(1)}, bf16[64,8,64]{2,1,0:T(8,128)(2,1)}, u32[]{:S(2)}) copy-start(bf16[64,8,64]{2,1,0:T(8,128)(2,1)} %param.13) | copy-start | bytes 196612
  62.2 12.8 %copy-start.4 = (bf16[64,64]{1,0:T(8,128)(2,1)S(1)}, bf16[64,64]{1,0:T(8,128)(2,1)}, u32[]{:S(2)}) copy-start(bf16[64,64]{1,0:T(8,128)(2,1)} %param.21) | copy-start | bytes 24580
  63.6 10.5 %all-to-all-start.3 = ((bf16[8,8,512]{2,0,1:T(8,128)(2,1)}), bf16[8,8,512]{2,0,1:T(8,128)(2,1)S(1)}, u32[]{:S(2)}, u32[]{:S(2)}) async-start(bf16[8,8,512]{2,0,1:T(8,128)(2,1)} %copy.94), calls=%async_computation.3 | async-start | bytes 131072 | tf_op jit(solution)/shard_map/all_to_all | solution.py:147
  67.0 34.3 %copy-start.1 = (f32[1024,128]{1,0:T(8,128)S(1)}, f32[1024,128]{1,0:T(8,128)}, u32[]{:S(2)}) copy-start(f32[1024,128]{1,0:T(8,128)} %param.22) | copy-start | bytes 1572868
  74.5 26.8 %copy-start.3 = (bf16[64,8,64]{2,1,0:T(8,128)(2,1)}, bf16[64,8,64]{2,1,0:T(8,128)(2,1)S(1)}, u32[]{:S(2)}) copy-start(bf16[64,8,64]{2,1,0:T(8,128)(2,1)S(1)} %get-tuple-element.71) | copy-start | bytes 196612
  76.2 12.7 %all-to-all-start.4 = ((bf16[8,64,256]{2,1,0:T(8,128)(2,1)}), bf16[8,64,256]{2,1,0:T(8,128)(2,1)S(1)}, u32[]{:S(2)}, u32[]{:S(2)}) async-start(bf16[8,64,256]{2,1,0:T(8,128)(2,1)} %broadcast_in_dim.51), calls=%async_computation.4 | async-start | bytes 524288 | tf_op jit(solution)/shard_map/all_to_all | solution.py:11
  90.1 32.0 %all-to-all-start.6 = ((f32[64,1,1]{2,1,0:T(1,128)}), f32[64,1,1]{2,1,0:T(1,128)S(1)}, u32[]{:S(2)}, u32[]{:S(2)}) async-start(f32[64,1,1]{2,1,0:T(1,128)} %broadcast_in_dim.52), calls=%async_computation.6 | async-start | bytes 65536 | tf_op jit(solution)/shard_map/all_to_all | solution.py:11
  101.3 41.6 %copy-start.6 = (f32[128]{0:T(128)S(1)}, f32[128]{0:T(128)}, u32[]{:S(2)}) copy-start(f32[128]{0:T(128)} %param.23) | copy-start | bytes 1540
  122.1 20.7 %all-to-all-start.5 = ((bf16[64,1,8,128]{3,2,1,0:T(8,128)(2,1)}), bf16[64,1,8,128]{3,2,1,0:T(8,128)(2,1)S(1)}, u32[]{:S(2)}, u32[]{:S(2)}) async-start(bf16[64,1,8,128]{3,2,1,0:T(8,128)(2,1)} %bitcast.35), calls=%async_computation.5 | async-start | bytes 262144 | tf_op jit(solution)/shard_map/all_to_all | solution.py:38
where the time goes:
time: 145 us; the launch traced here: 144 us
  starting transfers between devices  53 us (37%)
  waiting for transfers between devices  46 us (32%)
  matrix products  21.8 us (15%)
  local copies, waits for them, and re-layouts  10.9 us (8%)
  other arithmetic  8.25 us (6%)
  loops' own time  2.62 us (2%)
  between operations  1.66 us (1%)
    all_to_all x4, starting transfers between devices, from_everyone(): return lax.all_to_all(copies, axis, split_axis=0, concat_axis=0, tiled=True)  32.5 us
    all_to_all x4, waiting for transfers between devices, from_everyone(): return lax.all_to_all(copies, axis, split_axis=0, concat_axis=0, tiled=True)  23.3 us
    dot_general x4, matrix products, block_term(): jnp.einsum('icjd,cdp->ijp', outer_block, weight_cube, precision=lax.Preci...  14 us
    all_to_all x1, starting transfers between devices, summed_on_arrival(): lax.all_to_all(pieces, axis, split_axis=0, concat_axis=0, tiled=True)  10.3 us
    all_to_all x1, waiting for transfers between devices, summed_on_arrival(): lax.all_to_all(pieces, axis, split_axis=0, concat_axis=0, tiled=True)  9.59 us
    all_to_all x1, waiting for transfers between devices, local(): lax.all_to_all(update.reshape(-1, block_length * channel_width), 'res', s...  7.03 us
    all_to_all x1, starting transfers between devices, local(): lax.all_to_all(flat_rows, 'res', split_axis=0, concat_axis=1, tiled=True)  6.82 us
    all_to_all x1, waiting for transfers between devices, local(): lax.all_to_all(flat_rows, 'res', split_axis=0, concat_axis=1, tiled=True)  6.09 us
  transfers between devices with their start and end apart: 7, of which 6 were waited for; matrix products, arithmetic and copies ran while one was open for 17% of the time, Pallas kernels for 0%

commit v1 on v0

v1 whole, which is shorter than its diff:
```python
import functools
import math

import jax
import jax.numpy as jnp
from jax import lax
from jax.experimental import pallas as pl
from jax.experimental.pallas import tpu as pltpu
from jax.sharding import PartitionSpec as P

BF = jnp.bfloat16
F32 = jnp.float32
VMEM = pl.BlockSpec(memory_space=pltpu.VMEM)
SMEM = pl.BlockSpec(memory_space=pltpu.SMEM)


def dot(a, b):
    return jnp.dot(a, b, preferred_element_type=F32)


def dot_nt(a, b):
    return lax.dot_general(a, b, (((1,), (1,)), ((), ())), preferred_element_type=F32)


def dot_tn(a, b):
    return lax.dot_general(a, b, (((0,), (0,)), ((), ())), preferred_element_type=F32)


def dot_split(x, matrix):
    high = x.astype(BF)
    low = (x - high.astype(F32)).astype(BF)
    return dot(high, matrix) + dot(low, matrix)


def averager(width):
    row = lax.broadcasted_iota(jnp.int32, (width, width), 0) // 64
    col = lax.broadcasted_iota(jnp.int32, (width, width), 1) // 64
    return jnp.where(row == col, 1.0 / 64, 0.0).astype(BF)


def norm_groups(x, matrix):
    centred = x - dot_split(x, matrix)
    spread = dot_split(centred * centred, matrix)
    return centred * lax.rsqrt(spread + 1e-05)


def block_diagonal(weight):
    wide = jnp.concatenate([weight.astype(F32)] * 4, axis=1)
    full = jnp.concatenate([wide] * 4, axis=0)
    row = lax.broadcasted_iota(jnp.int32, full.shape, 0) // 64
    col = lax.broadcasted_iota(jnp.int32, full.shape, 1) // 64
    return jnp.where(row == col, full, 0.0).astype(BF)


def prepare_kernel(where_ref, count_ref, mask_ref, rows_ref, pair_ref, bias_w_ref, members_ref,
                   bias_out, send_out, own_out, rows_out):
    pair = pair_ref[...].astype(F32)
    pair = pair - jnp.mean(pair, axis=-1, keepdims=True)
    pair = pair * lax.rsqrt(jnp.mean(pair * pair, axis=-1, keepdims=True) + 1e-05)
    products = bias_w_ref[...][:, None, :] * pair[None, :, :]
    column = jnp.sum(products, axis=-1, keepdims=True).reshape(64, 1)
    row = lax.broadcasted_iota(jnp.int32, (64, 128), 0)
    lane = lax.broadcasted_iota(jnp.int32, (64, 128), 1)
    bias = jnp.sum(jnp.where(row == lane, column, 0.0), axis=0, keepdims=True)
    bias = bias + jnp.where(mask_ref[where_ref[0]] == 1, 0.0, -1000000.0)
    slot = lax.broadcasted_iota(jnp.int32, (1, 64), 1)
    weight = jnp.where(slot < count_ref[0], members_ref[...], 0).astype(F32)
    bias = jnp.where(lane[:1] < 64, bias, jnp.sum(weight))
    bias_out[...] = jnp.broadcast_to(bias[None], (64, 1, 128))

    rows = rows_ref[...].astype(F32)
    low = jnp.concatenate([rows[0:16], rows[16:32]], axis=-1)
    high = jnp.concatenate([rows[32:48], rows[48:64]], axis=-1)
    x = jnp.concatenate([low, high], axis=-1).reshape(128, 256)
    rows_out[...] = x
    normed = norm_groups(x, averager(256))
    own_out[...] = normed.astype(BF)
    block = normed.reshape(16, 8, 256).astype(BF)
    for peer in range(8):
        send_out[peer] = block


def project_kernel(own_ref, in_w_ref, out_w_ref, q_out, gate_out, k_out, v_out, o_out):
    weight = in_w_ref[...]
    own = own_ref[...]
    q_out[...] = dot(own, block_diagonal(weight[:, 0:64])) * (1.0 / math.sqrt(8))
    gate_out[...] = jax.nn.sigmoid(dot(own, block_diagonal(weight[:, 192:256])))
    k_out[...] = block_diagonal(weight[:, 64:128])
    v_out[...] = block_diagonal(weight[:, 128:192])
    o_out[...] = block_diagonal(out_w_ref[...])


GROUPS = 4


def attend_kernel(where_ref, count_ref, mask_ref, all_ref, bias_ref, q_ref, gate_ref, rows_ref,
                  k_w_ref, v_w_ref, o_w_ref, factor_ref, members_ref,
                  update_out, left_out, right_out,
                  x_scr, k_scr, v_scr, context_scr, norm_scr, left_scr):
    lane = lax.broadcasted_iota(jnp.int32, (64, 128), 1)
    bias = bias_ref[...]
    bias = jnp.where(lane < 64, bias, pltpu.roll(bias, 64, axis=1))
    for g in range(16):
        x_scr[g] = all_ref[:, g].astype(F32).reshape(64, 256).astype(BF)
    x = x_scr[...].reshape(1024, 256)
    k_scr[...] = dot(x, k_w_ref[...]).astype(BF).reshape(16, 64, 256)
    v_scr[...] = dot(x, v_w_ref[...]).astype(BF).reshape(16, 64, 256)
    diagonal = (lax.broadcasted_iota(jnp.int32, (16, 8, 128), 2) // 8
                == lax.broadcasted_iota(jnp.int32, (16, 8, 128), 0))

    def some_groups(step, carry):
        first = step * GROUPS
        parts = [(n, h) for n in range(GROUPS) for h in range(2)]
        scores = []
        for n, h in parts:
            start = pl.multiple_of((first + n) * 8, 8)
            q = q_ref[pl.ds(start, 8), h * 128:(h + 1) * 128]
            q = jnp.where(diagonal, q[None], 0.0).reshape(128, 128).astype(BF)
            k = k_scr[first + n, :, h * 128:(h + 1) * 128]
            scores.append(dot_nt(k, q) + bias)
        probs = []
        for s in scores:
            e = jnp.exp(s - jnp.max(s, axis=0, keepdims=True))
            probs.append((e * (1.0 / jnp.sum(e, axis=0, keepdims=True))).astype(BF))
        for (n, h), p in zip(parts, probs):
            start = pl.multiple_of((first + n) * 8, 8)
            v = v_scr[first + n, :, h * 128:(h + 1) * 128]
            full = dot_tn(p, v).reshape(16, 8, 128)
            context_scr[pl.ds(start, 8), h * 128:(h + 1) * 128] = jnp.sum(
                jnp.where(diagonal, full, 0.0), axis=0)
        return carry

    lax.fori_loop(0, 16 // GROUPS, some_groups, 0)

    gated = (gate_ref[...] * context_scr[...]).astype(BF)
    update = dot(gated, o_w_ref[...]).astype(BF).astype(F32)
    slot = (lax.broadcasted_iota(jnp.int32, (128, 256), 1) // 64 * 16
            + lax.broadcasted_iota(jnp.int32, (128, 256), 0) // 8)
    update = update * (slot < count_ref[0]).astype(F32)
    cube = update.reshape(16, 8, 256)
    for q in range(4):
        update_out[q * 16:(q + 1) * 16] = cube[:, :, q * 64:(q + 1) * 64].astype(BF)

    full_norm = norm_groups(rows_ref[...] + update, averager(256))
    norm_scr[0] = full_norm[:, :128]
    norm_scr[1] = full_norm[:, 128:]
    pieces = []
    for i in range(8):
        for half in range(2):
            z = norm_scr[half, pl.ds(i, 16, stride=8), :]
            pieces += [z, pltpu.roll(z, 64, axis=1)]
    tokens = jnp.concatenate(pieces, axis=0).astype(BF)

    factor = factor_ref[...].astype(F32)
    zero = jnp.zeros((64, 128), F32)
    right_w = jnp.concatenate([jnp.concatenate([factor[:, 32:64]] * 4, axis=1), zero], axis=0)
    right = dot(tokens, right_w.astype(BF))
    base = where_ref[1] * 8
    kept = []
    for j in range(8):
        keep = (mask_ref[base + j]).astype(F32)
        kept.append(right[j * 64:(j + 1) * 64] * keep)
    for quad in range(2):
        a, b, c, d = kept[quad * 4:quad * 4 + 4]
        r = jnp.where(lane < 64, jnp.where(lane < 32, a, b), jnp.where(lane < 96, c, d))
        right_out[:, quad * 128:(quad + 1) * 128] = r.astype(BF)

    left_w = jnp.concatenate([factor.T[0:32], jnp.zeros((32, 64), F32)], axis=1).astype(BF)
    left = dot_nt(left_w, tokens)
    members = members_ref[...]
    members = jnp.concatenate([members, members], axis=1)
    lane1 = lax.broadcasted_iota(jnp.int32, (1, 128), 1)
    weight = jnp.where(lane1 % 64 < count_ref[0], members, 0).astype(F32)
    lane32 = lax.broadcasted_iota(jnp.int32, (32, 128), 1)
    for pair in range(4):
        both = left[:, pair * 128:(pair + 1) * 128]
        turned = pltpu.roll(both, 64, axis=1)
        for odd in range(2):
            i = pair * 2 + odd
            keep = (mask_ref[base + i]).astype(F32)
            mine = jnp.where((lane32 < 64) == (odd == 0), both, turned)
            left_scr[i * 32:(i + 1) * 32, :] = mine * (weight * keep)
    rows = []
    lane8 = lax.broadcasted_iota(jnp.int32, (8, 128), 1)
    for c in range(16):
        rows.append(jnp.where(lane8 < 64, left_scr[pl.ds(2 * c, 8, stride=32), :],
                              left_scr[pl.ds(2 * c + 1, 8, stride=32), :]))
    block = jnp.concatenate(rows, axis=0).astype(BF)
    for peer in range(8):
        left_out[peer] = block


def outer_kernel(left_ref, right_ref, weight_ref, out_ref, outer_scr, part_scr):
    right = right_ref[...]
    zero = jnp.zeros_like(right)
    both = jnp.concatenate([jnp.concatenate([right, zero], axis=1),
                            jnp.concatenate([zero, right], axis=1)], axis=0)
    outer_scr[...] = dot(left_ref[...].reshape(1024, 128), both).reshape(8, 16, 8, 512)
    weight = weight_ref[...].astype(BF)
    lane = lax.broadcasted_iota(jnp.int32, (64, 128), 1)
    for quad in range(2):
        rows = [[] for _ in range(4)]
        for m in range(8):
            pieces = []
            for k in range(4):
                c, odd = 2 * m + k // 2, k % 2
                lanes = odd * 256 + quad * 128
                pieces.append(outer_scr[:, c, :, lanes:lanes + 128].reshape(64, 128))
            for j in range(4):
                turned = [pltpu.roll(p, (k - j) * 32 % 128, axis=1) if k != j else p
                          for k, p in enumerate(pieces)]
                low = jnp.where(lane < 32, turned[0], turned[1])
                high = jnp.where(lane < 96, turned[2], turned[3])
                rows[j].append(jnp.where(lane < 64, low, high).astype(BF))
        for j in range(4):
            part = dot(jnp.concatenate(rows[j], axis=1), weight)
            part_scr[pl.ds(quad * 4 + j, 64, stride=8), :] = part
    out_ref[...] = part_scr[...].reshape(64, 8, 128).astype(BF)


def call(kernel, outs, specs, scratch=(), flops=0):
    return pl.pallas_call(
        kernel,
        out_shape=[jax.ShapeDtypeStruct(shape, kind) for shape, kind in outs],
        in_specs=specs,
        out_specs=[VMEM] * len(outs),
        scratch_shapes=[pltpu.VMEM(shape, kind) for shape, kind in scratch],
        cost_estimate=pl.CostEstimate(flops=flops, bytes_accessed=1 << 20, transcendentals=0),
    )


def local(
    alignment_rows,
    pair_features,
    sequence_block_count,
    cluster_member_count,
    residue_present_mask,
    attention_in_weight,
    attention_out_weight,
    pair_bias_weight,
    outer_factor_weight,
    outer_output_weight,
    outer_product_bias,
):
    here = jnp.stack([lax.axis_index("seq"), lax.axis_index("res")]).astype(jnp.int32)
    members = cluster_member_count.reshape(1, 64)
    bias_send, rows_send, own_norm, own_rows = call(
        prepare_kernel,
        [((64, 1, 128), F32), ((8, 16, 8, 256), BF), ((128, 256), BF), ((128, 256), F32)],
        [SMEM] * 3 + [VMEM] * 4,
    )(here, sequence_block_count, residue_present_mask, alignment_rows,
      pair_features.reshape(8, 128), pair_bias_weight.T, members)
    rows_all = lax.all_to_all(rows_send, "res", split_axis=0, concat_axis=0, tiled=True)
    bias_all = lax.all_to_all(bias_send, "seq", split_axis=0, concat_axis=0, tiled=True)
    bias_all = bias_all.reshape(64, 128)
    queries, gate, k_w, v_w, o_w = call(
        project_kernel,
        [((128, 256), F32), ((128, 256), F32)] + [((256, 256), BF)] * 3,
        [VMEM] * 3,
        flops=1 << 30,
    )(own_norm, attention_in_weight, attention_out_weight)
    row_attention_update, left_send, right = call(
        attend_kernel,
        [((64, 8, 64), BF), ((8, 128, 128), BF), ((64, 256), BF)],
        [SMEM] * 3 + [VMEM] * 10,
        [((16, 64, 256), BF)] * 3
        + [((128, 256), F32), ((2, 128, 128), F32), ((256, 128), F32)],
    )(here, sequence_block_count, residue_present_mask, rows_all, bias_all, queries, gate,
      own_rows, k_w, v_w, o_w, outer_factor_weight, members)
    left_all = lax.all_to_all(left_send, "res", split_axis=0, concat_axis=0, tiled=True)
    (partial,) = call(
        outer_kernel,
        [((64, 8, 128), BF)],
        [VMEM] * 3,
        [((8, 16, 8, 512), F32), ((512, 128), F32)],
    )(left_all, right, outer_output_weight)
    arrived = lax.all_to_all(partial, "seq", split_axis=0, concat_axis=0, tiled=True)
    summed = arrived.astype(F32).sum(axis=0)
    weight_sum = jnp.sum(bias_all[:, 64])
    pair_update = (summed / weight_sum + outer_product_bias).astype(BF)
    return (row_attention_update, pair_update[None])


def solution(mesh):
    return jax.shard_map(
        local,
        mesh=mesh,
        in_specs=(
            P("seq", "res", None),
            P("res", "seq", None),
            P("seq"),
            P("seq"),
            P(),
            P(),
            P(),
            P(),
            P(),
            P(),
            P(),
        ),
        out_specs=(P("seq", "res", None), P("seq", "res", None)),
        check_vma=False,
    )
```

time: 145 us -> 96 us (0.66)
  starting transfers between devices: 53 us -> 11.6 us
  blocking collectives: 0 us -> 40.5 us
  matrix products: 21.8 us -> 0 us
  waiting for transfers between devices: 46 us -> 25.7 us
  Pallas kernels: 0 us -> 12.8 us
  local copies, waits for them, and re-layouts: 10.9 us -> 0.8 us
  other arithmetic: 8.25 us -> 2.61 us
  loops' own time: 2.62 us -> 0 us
    all_to_all x7 -> x2, starting transfers between devices: 53 us -> 11.6 us  [the longest x1 6.82 us: local(): lax.all_to_all(rows_send, 'res', split_axis=0, concat_axis=0, tiled=True)]
    all_to_all x0 -> x2, blocking collectives: none -> 40.5 us  [the longest x1 24.3 us: local(): lax.all_to_all(bias_send, 'seq', split_axis=0, concat_axis=0, tiled=True)]
    all_to_all x7 -> x2, waiting for transfers between devices: 46 us -> 25.7 us  [the longest x1 16 us: local(): lax.all_to_all(rows_send, 'res', split_axis=0, concat_axis=0, tiled=True)]
    dot_general x13 -> x0, matrix products: 19.5 us -> none  [the longest x4 14 us: block_term(): jnp.einsum('icjd,cdp->ijp', outer_block, weight_cube, precision=lax.Preci...]
    pallas_call x0 -> x4, Pallas kernels: none -> 12.8 us  [the longest x1 5.62 us: local(): call(attend_kernel, [((64, 8, 64), BF), ((8, 128, 128), BF), ((64, 256),...]
    reduce_sum x9 -> x2, other arithmetic: 4.61 us -> 0.76 us  [the longest x1 0.69 us: local(): weight_sum = jnp.sum(bias_all[:, 64])]
    all_to_all x6 -> x0, local copies, waits for them, and re-layouts: 3.29 us -> none  [the longest x1 1.67 us: local(): lax.all_to_all(flat_rows, 'res', split_axis=0, concat_axis=1, tiled=True)]
    broadcast_in_dim x4 -> x0, local copies, waits for them, and re-layouts: 2.7 us -> none  [from_everyone(): copies = jnp.broadcast_to(shard, (lax.axis_size(axis), *shard.shape))]
  transfers between devices with their start and end apart: 7 -> 2, of which waited for: 6 -> 2; matrix products, arithmetic and copies ran while one was open for 17% -> 1% of each run, Pallas kernels for 0% -> 2%
where the time goes in v1:
time: 96 us; the launch traced here: 95.4 us
  blocking collectives  40.5 us (42%)
  waiting for transfers between devices  25.7 us (27%)
  Pallas kernels  12.8 us (13%)
  starting transfers between devices  11.6 us (12%)
  other arithmetic  2.61 us (3%)
  between operations  1.31 us (1%)
    all_to_all x1, blocking collectives, local(): lax.all_to_all(bias_send, 'seq', split_axis=0, concat_axis=0, tiled=True)  24.3 us
    all_to_all x1, blocking collectives, local(): lax.all_to_all(left_send, 'res', split_axis=0, concat_axis=0, tiled=True)  16.2 us
    all_to_all x1, waiting for transfers between devices, local(): lax.all_to_all(rows_send, 'res', split_axis=0, concat_axis=0, tiled=True)  16 us
    all_to_all x1, waiting for transfers between devices, local(): lax.all_to_all(partial, 'seq', split_axis=0, concat_axis=0, tiled=True)  9.75 us
    all_to_all x1, starting transfers between devices, local(): lax.all_to_all(rows_send, 'res', split_axis=0, concat_axis=0, tiled=True)  6.82 us
    pallas_call x1, Pallas kernels, local(): call(attend_kernel, [((64, 8, 64), BF), ((8, 128, 128), BF), ((64, 256),...  5.62 us
    all_to_all x1, starting transfers between devices, local(): lax.all_to_all(partial, 'seq', split_axis=0, concat_axis=0, tiled=True)  4.8 us
    pallas_call x1, Pallas kernels, local(): call(outer_kernel, [((64, 8, 128), BF)], [VMEM] * 3, [((8, 16, 8, 512), F...  3.08 us
  transfers between devices with their start and end apart: 2, of which 2 were waited for; matrix products, arithmetic and copies ran while one was open for 1% of the time, Pallas kernels for 2%

profile of v1, /device:TPU:1, one launch (start us, length us, event | category | flops | bytes accessed | tf_op | source)
XLA Modules:
  0.0 95.4 jit_solution(13167210135674365233)
XLA Ops:
  1.3 0.7 pad_add_fusion.where_ref
  1.9 2.2 %shard_map.122 = (f32[64,1,128]{2,1,0:T(1,128)}, bf16[8,16,8,256]{3,2,1,0:T(8,128)(2,1)}, bf16[128,256]{1,0:T(8,128)(2,1)}, f32[128,256]{1,0:T(8,128)}) custom-call(s32[2]{0:T(128)} %pad_add_fusion.where_ref, s32[1]{0:T(128)S(6)} %copy.14.count_ref, s32[64]{0:T(128)} %mask_ref.3, bf16[64,8,64]{2,1,0:T(8,128)(2,1)} %rows_ref.1, bf16[8,128]{1,0:T(8,128)(2,1)} %bitcast.13, ...), custom_call_target="tpu_custom_call" | custom-call | bytes 1048576 | tf_op jit(solution)/shard_map/pallas_call | solution.py:247
  4.1 24.3 %all_to_all.20 = f32[64,1,128]{2,1,0:T(1,128)} all-to-all(f32[64,1,128]{2,1,0:T(1,128)} %get-tuple-element.15), channel_id=1, replica_groups=mesh['seq'=64,'res'=8] {'seq'}, dimensions={0} | all-to-all | bytes 65536 | tf_op jit(solution)/shard_map/all_to_all | solution.py:254
  28.4 6.8 %all-to-all-start = ((bf16[8,16,8,256]{3,2,1,0:T(8,128)(2,1)}), bf16[8,16,8,256]{3,2,1,0:T(8,128)(2,1)S(1)}, u32[]{:S(2)}, u32[]{:S(2)}) async-start(bf16[8,16,8,256]{3,2,1,0:T(8,128)(2,1)} %get-tuple-element.14), calls=%async_computation | async-start | bytes 1048576 | tf_op jit(solution)/shard_map/all_to_all | solution.py:253
  35.2 2.0 %shard_map.123 = (f32[128,256]{1,0:T(8,128)}, f32[128,256]{1,0:T(8,128)}, bf16[256,256]{1,0:T(8,128)(2,1)}, bf16[256,256]{1,0:T(8,128)(2,1)}, bf16[256,256]{1,0:T(8,128)(2,1)}) custom-call(bf16[128,256]{1,0:T(8,128)(2,1)} %get-tuple-element.16.own_ref, bf16[64,256]{1,0:T(8,128)(2,1)} %in_w_ref.1, bf16[64,64]{1,0:T(8,128)(2,1)} %out_w_ref.1), custom_call_target="tpu_custom_call" | custom-call | flops 1073741824 | bytes 1048576 | tf_op jit(solution)/shard_map/pallas_call | solution.py:256
  37.2 16.0 %all-to-all-done.all_ref = bf16[8,16,8,256]{3,2,1,0:T(8,128)(2,1)S(1)} async-done(((bf16[8,16,8,256]{3,2,1,0:T(8,128)(2,1)}), bf16[8,16,8,256]{3,2,1,0:T(8,128)(2,1)S(1)}, u32[]{:S(2)}, u32[]{:S(2)}) %all-to-all-start) | async-done | bytes 524320 | tf_op jit(solution)/shard_map/all_to_all | solution.py:253
  53.2 0.0 copy-start
  53.2 0.8 copy-done
  53.9 5.6 %shard_map.124 = (bf16[64,8,64]{2,1,0:T(8,128)(2,1)}, bf16[8,128,128]{2,1,0:T(8,128)(2,1)}, bf16[64,256]{1,0:T(8,128)(2,1)}) custom-call(s32[2]{0:T(128)} %pad_add_fusion.where_ref, s32[1]{0:T(128)S(6)} %copy.14.count_ref, s32[64]{0:T(128)} %mask_ref.3, bf16[8,16,8,256]{3,2,1,0:T(8,128)(2,1)} %copy-done, f32[64,128]{1,0:T(8,128)} %bitcast.10, ...), custom_call_target="tpu_custom_call" | custom-call | bytes 1048576 | tf_op jit(solution)/shard_map/pallas_call | solution.py:262
  59.6 16.2 %all_to_all.21.left_ref = bf16[8,128,128]{2,1,0:T(8,128)(2,1)} all-to-all(bf16[8,128,128]{2,1,0:T(8,128)(2,1)} %get-tuple-element.24), channel_id=1, replica_groups=mesh['seq'=64,'res'=8] {'res'}, dimensions={0} | all-to-all | bytes 524288 | tf_op jit(solution)/shard_map/all_to_all | solution.py:270
  75.8 3.1 %shard_map.125 = bf16[64,8,128]{2,1,0:T(8,128)(2,1)} custom-call(bf16[8,128,128]{2,1,0:T(8,128)(2,1)} %all_to_all.21.left_ref, bf16[64,256]{1,0:T(8,128)(2,1)} %get-tuple-element.25.right_ref, f32[1024,128]{1,0:T(8,128)} %weight_ref.1), custom_call_target="tpu_custom_call" | custom-call | bytes 1048576 | tf_op jit(solution)/shard_map/pallas_call | solution.py:271
  78.9 0.0 copy-start.1
  78.9 4.8 %all-to-all-start.3 = ((bf16[64,8,128]{2,1,0:T(8,128)(2,1)}), bf16[64,8,128]{2,1,0:T(8,128)(2,1)S(1)}, u32[]{:S(2)}, u32[]{:S(2)}) async-start(bf16[64,8,128]{2,1,0:T(8,128)(2,1)} %shard_map.125), calls=%async_computation.3 | async-start | bytes 262144 | tf_op jit(solution)/shard_map/all_to_all | solution.py:277
  83.7 0.0 copy-done.1
  83.7 0.7 slice_reduce_fusion
  84.4 0.0 copy-start.2
  84.4 9.7 %all-to-all-done.3 = bf16[64,8,128]{2,1,0:T(8,128)(2,1)S(1)} async-done(((bf16[64,8,128]{2,1,0:T(8,128)(2,1)}), bf16[64,8,128]{2,1,0:T(8,128)(2,1)S(1)}, u32[]{:S(2)}, u32[]{:S(2)}) %all-to-all-start.3) | async-done | bytes 131104 | tf_op jit(solution)/shard_map/all_to_all | solution.py:277
  94.1 0.1 convert_reduce_fusion
  94.2 0.0 copy-done.2
  94.2 1.2 %fusion = bf16[1,8,128]{2,1,0:T(8,128)(2,1)} fusion(f32[8,128]{1,0:T(8,128)S(1)} %convert_reduce_fusion, f32[128]{0:T(128)S(1)} %copy-done.2, f32[]{:T(128)} %slice_reduce_fusion), kind=kLoop, calls=%fused_computation.3 | loop fusion | flops 3072 | bytes 6660 | tf_op jit(solution)/shard_map/convert_element_type | solution.py:280
Async XLA Ops:
  28.4 24.8 %all-to-all-start = ((bf16[8,16,8,256]{3,2,1,0:T(8,128)(2,1)}), bf16[8,16,8,256]{3,2,1,0:T(8,128)(2,1)S(1)}, u32[]{:S(2)}, u32[]{:S(2)}) async-start(bf16[8,16,8,256]{3,2,1,0:T(8,128)(2,1)} %get-tuple-element.14), calls=%async_computation | async-start | bytes 1048576 | tf_op jit(solution)/shard_map/all_to_all | solution.py:253
  53.2 0.8 copy-start
  78.9 4.8 %copy-start.1 = (f32[64,1,128]{2,1,0:T(1,128)S(1)}, f32[64,1,128]{2,1,0:T(1,128)}, u32[]{:S(2)}) copy-start(f32[64,1,128]{2,1,0:T(1,128)} %all_to_all.20) | copy-start | bytes 98308
  78.9 15.3 %all-to-all-start.3 = ((bf16[64,8,128]{2,1,0:T(8,128)(2,1)}), bf16[64,8,128]{2,1,0:T(8,128)(2,1)S(1)}, u32[]{:S(2)}, u32[]{:S(2)}) async-start(bf16[64,8,128]{2,1,0:T(8,128)(2,1)} %shard_map.125), calls=%async_computation.3 | async-start | bytes 262144 | tf_op jit(solution)/shard_map/all_to_all | solution.py:277
  84.4 9.8 %copy-start.2 = (f32[128]{0:T(128)S(1)}, f32[128]{0:T(128)}, u32[]{:S(2)}) copy-start(f32[128]{0:T(128)} %param.21) | copy-start | bytes 1540

commit v2 on v1

--- a/solution.py
+++ b/solution.py
@@ -52,7 +52,7 @@
     return jnp.where(row == col, full, 0.0).astype(BF)
 
 
-def prepare_kernel(where_ref, count_ref, mask_ref, rows_ref, pair_ref, bias_w_ref, members_ref,
+def prepare_kernel(count_ref, mask_ref, rows_ref, pair_ref, bias_w_ref, members_ref,
                    bias_out, send_out, own_out, rows_out):
     pair = pair_ref[...].astype(F32)
     pair = pair - jnp.mean(pair, axis=-1, keepdims=True)
@@ -62,7 +62,7 @@
     row = lax.broadcasted_iota(jnp.int32, (64, 128), 0)
     lane = lax.broadcasted_iota(jnp.int32, (64, 128), 1)
     bias = jnp.sum(jnp.where(row == lane, column, 0.0), axis=0, keepdims=True)
-    bias = bias + jnp.where(mask_ref[where_ref[0]] == 1, 0.0, -1000000.0)
+    bias = bias + jnp.where(mask_ref[lax.axis_index("seq")] == 1, 0.0, -1000000.0)
     slot = lax.broadcasted_iota(jnp.int32, (1, 64), 1)
     weight = jnp.where(slot < count_ref[0], members_ref[...], 0).astype(F32)
     bias = jnp.where(lane[:1] < 64, bias, jnp.sum(weight))
@@ -93,7 +93,7 @@
 GROUPS = 4
 
 
-def attend_kernel(where_ref, count_ref, mask_ref, all_ref, bias_ref, q_ref, gate_ref, rows_ref,
+def attend_kernel(count_ref, mask_ref, all_ref, bias_ref, q_ref, gate_ref, rows_ref,
                   k_w_ref, v_w_ref, o_w_ref, factor_ref, members_ref,
                   update_out, left_out, right_out,
                   x_scr, k_scr, v_scr, context_scr, norm_scr, left_scr):
@@ -155,7 +155,7 @@
     zero = jnp.zeros((64, 128), F32)
     right_w = jnp.concatenate([jnp.concatenate([factor[:, 32:64]] * 4, axis=1), zero], axis=0)
     right = dot(tokens, right_w.astype(BF))
-    base = where_ref[1] * 8
+    base = lax.axis_index("res") * 8
     kept = []
     for j in range(8):
         keep = (mask_ref[base + j]).astype(F32)
@@ -218,7 +218,7 @@
     out_ref[...] = part_scr[...].reshape(64, 8, 128).astype(BF)
 
 
-def call(kernel, outs, specs, scratch=(), flops=0):
+def call(kernel, outs, specs, scratch=(), flops=0, limit=8):
     return pl.pallas_call(
         kernel,
         out_shape=[jax.ShapeDtypeStruct(shape, kind) for shape, kind in outs],
@@ -226,6 +226,7 @@
         out_specs=[VMEM] * len(outs),
         scratch_shapes=[pltpu.VMEM(shape, kind) for shape, kind in scratch],
         cost_estimate=pl.CostEstimate(flops=flops, bytes_accessed=1 << 20, transcendentals=0),
+        compiler_params=pltpu.CompilerParams(vmem_limit_bytes=limit << 20),
     )
 
 
@@ -242,16 +243,15 @@
     outer_output_weight,
     outer_product_bias,
 ):
-    here = jnp.stack([lax.axis_index("seq"), lax.axis_index("res")]).astype(jnp.int32)
     members = cluster_member_count.reshape(1, 64)
     bias_send, rows_send, own_norm, own_rows = call(
         prepare_kernel,
         [((64, 1, 128), F32), ((8, 16, 8, 256), BF), ((128, 256), BF), ((128, 256), F32)],
-        [SMEM] * 3 + [VMEM] * 4,
-    )(here, sequence_block_count, residue_present_mask, alignment_rows,
+        [SMEM] * 2 + [VMEM] * 4,
+    )(sequence_block_count, residue_present_mask, alignment_rows,
       pair_features.reshape(8, 128), pair_bias_weight.T, members)
+    bias_all = lax.all_to_all(bias_send, "seq", split_axis=0, concat_axis=0, tiled=True)
     rows_all = lax.all_to_all(rows_send, "res", split_axis=0, concat_axis=0, tiled=True)
-    bias_all = lax.all_to_all(bias_send, "seq", split_axis=0, concat_axis=0, tiled=True)
     bias_all = bias_all.reshape(64, 128)
     queries, gate, k_w, v_w, o_w = call(
         project_kernel,
@@ -262,10 +262,10 @@
     row_attention_update, left_send, right = call(
         attend_kernel,
         [((64, 8, 64), BF), ((8, 128, 128), BF), ((64, 256), BF)],
-        [SMEM] * 3 + [VMEM] * 10,
+        [SMEM] * 2 + [VMEM] * 10,
         [((16, 64, 256), BF)] * 3
         + [((128, 256), F32), ((2, 128, 128), F32), ((256, 128), F32)],
-    )(here, sequence_block_count, residue_present_mask, rows_all, bias_all, queries, gate,
+    )(sequence_block_count, residue_present_mask, rows_all, bias_all, queries, gate,
       own_rows, k_w, v_w, o_w, outer_factor_weight, members)
     left_all = lax.all_to_all(left_send, "res", split_axis=0, concat_axis=0, tiled=True)
     (partial,) = call(

time: 96 us -> 91.8 us (0.956)
  Pallas kernels: 12.8 us -> 8.77 us
  blocking collectives: 40.5 us -> 38.7 us
  waiting for transfers between devices: 25.7 us -> 27.3 us
    pallas_call x1, Pallas kernels: 1.96 us -> 0.34 us  [local(): call(project_kernel, [((128, 256), F32), ((128, 256), F32)] + [((256, 256...]
    all_to_all x1, waiting for transfers between devices: 16 us -> 17.6 us  [local(): lax.all_to_all(rows_send, 'res', split_axis=0, concat_axis=0, tiled=True)]
    all_to_all x1, blocking collectives: 16.2 us -> 14.7 us  [local(): lax.all_to_all(left_send, 'res', split_axis=0, concat_axis=0, tiled=True)]
    pallas_call x1, Pallas kernels: 3.08 us -> 1.95 us  [local(): call(outer_kernel, [((64, 8, 128), BF)], [VMEM] * 3, [((8, 16, 8, 512), F...]
  transfers between devices with their start and end apart: 2 -> 2, of which waited for: 2 -> 2; matrix products, arithmetic and copies ran while one was open for 1% -> 1% of each run, Pallas kernels for 2% -> 0%
where the time goes in v2:
time: 91.8 us; the launch traced here: 91.4 us
  blocking collectives  38.7 us (42%)
  waiting for transfers between devices  27.3 us (30%)
  starting transfers between devices  11.6 us (13%)
  Pallas kernels  8.77 us (10%)
  other arithmetic  2.1 us (2%)
  local copies, waits for them, and re-layouts  1.58 us (2%)
  between operations  1.38 us (2%)
    all_to_all x1, blocking collectives, local(): lax.all_to_all(bias_send, 'seq', split_axis=0, concat_axis=0, tiled=True)  23.9 us
    all_to_all x1, waiting for transfers between devices, local(): lax.all_to_all(rows_send, 'res', split_axis=0, concat_axis=0, tiled=True)  17.6 us
    all_to_all x1, blocking collectives, local(): lax.all_to_all(left_send, 'res', split_axis=0, concat_axis=0, tiled=True)  14.7 us
    all_to_all x1, waiting for transfers between devices, local(): lax.all_to_all(partial, 'seq', split_axis=0, concat_axis=0, tiled=True)  9.69 us
    all_to_all x1, starting transfers between devices, local(): lax.all_to_all(rows_send, 'res', split_axis=0, concat_axis=0, tiled=True)  6.95 us
    pallas_call x1, Pallas kernels, local(): call(attend_kernel, [((64, 8, 64), BF), ((8, 128, 128), BF), ((64, 256),...  4.71 us
    all_to_all x1, starting transfers between devices, local(): lax.all_to_all(partial, 'seq', split_axis=0, concat_axis=0, tiled=True)  4.66 us
    pallas_call x1, Pallas kernels, local(): call(outer_kernel, [((64, 8, 128), BF)], [VMEM] * 3, [((8, 16, 8, 512), F...  1.95 us
  transfers between devices with their start and end apart: 2, of which 2 were waited for; matrix products, arithmetic and copies ran while one was open for 1% of the time, Pallas kernels for 0%

profile of v2, /device:TPU:1, one launch (start us, length us, event | category | flops | bytes accessed | tf_op | source)
XLA Modules:
  0.0 91.4 jit_solution(6170120378394954597)
XLA Ops:
  0.6 0.0 copy-start.3
  1.3 0.0 copy-start.4
  1.3 0.0 copy-start.5
  1.3 0.0 copy-start.6
  1.3 0.0 copy-done.3
  1.3 0.6 copy-done.4
  2.0 0.0 copy-done.5
  2.0 0.0 copy-done.6
  2.0 0.0 copy-start.1
  2.0 0.9 copy-done.1
  2.9 1.8 %shard_map.122 = (f32[64,1,128]{2,1,0:T(1,128)S(1)}, bf16[8,16,8,256]{3,2,1,0:T(8,128)(2,1)}, bf16[128,256]{1,0:T(8,128)(2,1)S(1)}, f32[128,256]{1,0:T(8,128)S(1)}) custom-call(s32[1]{0:T(128)S(6)} %copy.14.count_ref, s32[64]{0:T(128)S(1)} %copy-done.5, bf16[64,8,64]{2,1,0:T(8,128)(2,1)S(1)} %copy-done.1, bf16[8,128]{1,0:T(8,128)(2,1)S(1)} %bitcast.11, ...), custom_call_target="tpu_custom_call" | custom-call | bytes 1048576 | tf_op jit(solution)/shard_map/pallas_call | solution.py:247
  4.7 23.9 %all_to_all.20 = f32[64,1,128]{2,1,0:T(1,128)S(1)} all-to-all(f32[64,1,128]{2,1,0:T(1,128)S(1)} %get-tuple-element.15), channel_id=1, replica_groups=mesh['seq'=64,'res'=8] {'seq'}, dimensions={0} | all-to-all | bytes 65536 | tf_op jit(solution)/shard_map/all_to_all | solution.py:253
  28.6 0.0 copy-start.7
  28.6 0.0 copy-start.8
  28.6 7.0 %all-to-all-start = ((bf16[8,16,8,256]{3,2,1,0:T(8,128)(2,1)}), bf16[8,16,8,256]{3,2,1,0:T(8,128)(2,1)S(1)}, u32[]{:S(2)}, u32[]{:S(2)}) async-start(bf16[8,16,8,256]{3,2,1,0:T(8,128)(2,1)} %get-tuple-element.14), calls=%async_computation | async-start | bytes 1048576 | tf_op jit(solution)/shard_map/all_to_all | solution.py:254
  35.6 0.0 copy-done.7
  35.6 0.0 copy-done.8
  35.6 0.0 copy-start.2
  35.6 0.3 shard_map.123
  35.9 17.6 %all-to-all-done.all_ref = bf16[8,16,8,256]{3,2,1,0:T(8,128)(2,1)S(1)} async-done(((bf16[8,16,8,256]{3,2,1,0:T(8,128)(2,1)}), bf16[8,16,8,256]{3,2,1,0:T(8,128)(2,1)S(1)}, u32[]{:S(2)}, u32[]{:S(2)}) %all-to-all-start) | async-done | bytes 524320 | tf_op jit(solution)/shard_map/all_to_all | solution.py:254
  53.5 0.0 copy-done.2
  53.5 4.7 %shard_map.124 = (bf16[64,8,64]{2,1,0:T(8,128)(2,1)}, bf16[8,128,128]{2,1,0:T(8,128)(2,1)S(1)}, bf16[64,256]{1,0:T(8,128)(2,1)S(1)}) custom-call(s32[1]{0:T(128)S(6)} %copy.14.count_ref, s32[64]{0:T(128)S(1)} %copy-done.5, bf16[8,16,8,256]{3,2,1,0:T(8,128)(2,1)S(1)} %all-to-all-done.all_ref, f32[64,128]{1,0:T(8,128)S(1)} %bitcast.8, ...), custom_call_target="tpu_custom_call" | custom-call | bytes 1048576 | tf_op jit(solution)/shard_map/pallas_call | solution.py:262
  58.2 0.0 copy-start
  58.2 14.7 %all_to_all.21.left_ref = bf16[8,128,128]{2,1,0:T(8,128)(2,1)S(1)} all-to-all(bf16[8,128,128]{2,1,0:T(8,128)(2,1)S(1)} %get-tuple-element.24), channel_id=1, replica_groups=mesh['seq'=64,'res'=8] {'res'}, dimensions={0} | all-to-all | bytes 524288 | tf_op jit(solution)/shard_map/all_to_all | solution.py:270
  72.9 0.0 copy-done
  72.9 1.9 %shard_map.125 = bf16[64,8,128]{2,1,0:T(8,128)(2,1)} custom-call(bf16[8,128,128]{2,1,0:T(8,128)(2,1)S(1)} %all_to_all.21.left_ref, bf16[64,256]{1,0:T(8,128)(2,1)S(1)} %get-tuple-element.25.right_ref, f32[1024,128]{1,0:T(8,128)S(1)} %copy-done), custom_call_target="tpu_custom_call" | custom-call | bytes 1048576 | tf_op jit(solution)/shard_map/pallas_call | solution.py:271
  74.9 4.7 %all-to-all-start.3 = ((bf16[64,8,128]{2,1,0:T(8,128)(2,1)}), bf16[64,8,128]{2,1,0:T(8,128)(2,1)S(1)}, u32[]{:S(2)}, u32[]{:S(2)}) async-start(bf16[64,8,128]{2,1,0:T(8,128)(2,1)} %shard_map.125), calls=%async_computation.3 | async-start | bytes 262144 | tf_op jit(solution)/shard_map/all_to_all | solution.py:277
  79.6 0.8 slice_reduce_fusion
  80.3 0.0 copy-start.9
  80.3 9.7 %all-to-all-done.3 = bf16[64,8,128]{2,1,0:T(8,128)(2,1)S(1)} async-done(((bf16[64,8,128]{2,1,0:T(8,128)(2,1)}), bf16[64,8,128]{2,1,0:T(8,128)(2,1)S(1)}, u32[]{:S(2)}, u32[]{:S(2)}) %all-to-all-start.3) | async-done | bytes 131104 | tf_op jit(solution)/shard_map/all_to_all | solution.py:277
  90.0 0.1 convert_reduce_fusion
  90.1 0.0 copy-done.9
  90.1 1.3 %fusion = bf16[1,8,128]{2,1,0:T(8,128)(2,1)} fusion(f32[8,128]{1,0:T(8,128)S(1)} %convert_reduce_fusion, f32[128]{0:T(128)S(1)} %copy-done.9, f32[]{:T(128)} %slice_reduce_fusion), kind=kLoop, calls=%fused_computation.3 | loop fusion | flops 3072 | bytes 6660 | tf_op jit(solution)/shard_map/convert_element_type | solution.py:280
Async XLA Ops:
  0.6 0.7 copy-start.3
  1.3 0.7 copy-start.4
  1.3 0.7 copy-start.5
  1.3 0.7 copy-start.6
  2.0 0.9 copy-start.1
  28.6 7.0 %copy-start.7 = (bf16[64,256]{1,0:T(8,128)(2,1)S(1)}, bf16[64,256]{1,0:T(8,128)(2,1)}, u32[]{:S(2)}) copy-start(bf16[64,256]{1,0:T(8,128)(2,1)} %in_w_ref.1) | copy-start | bytes 98308
  28.6 7.0 %copy-start.8 = (bf16[64,64]{1,0:T(8,128)(2,1)S(1)}, bf16[64,64]{1,0:T(8,128)(2,1)}, u32[]{:S(2)}) copy-start(bf16[64,64]{1,0:T(8,128)(2,1)} %out_w_ref.1) | copy-start | bytes 24580
  28.6 24.9 %all-to-all-start = ((bf16[8,16,8,256]{3,2,1,0:T(8,128)(2,1)}), bf16[8,16,8,256]{3,2,1,0:T(8,128)(2,1)S(1)}, u32[]{:S(2)}, u32[]{:S(2)}) async-start(bf16[8,16,8,256]{3,2,1,0:T(8,128)(2,1)} %get-tuple-element.14), calls=%async_computation | async-start | bytes 1048576 | tf_op jit(solution)/shard_map/all_to_all | solution.py:254
  35.6 17.9 %copy-start.2 = (bf16[64,64]{1,0:T(8,128)(2,1)S(1)}, bf16[64,64]{1,0:T(8,128)(2,1)}, u32[]{:S(2)}) copy-start(bf16[64,64]{1,0:T(8,128)(2,1)} %factor_ref.1) | copy-start | bytes 24580
  58.2 14.7 %copy-start = (f32[1024,128]{1,0:T(8,128)S(1)}, f32[1024,128]{1,0:T(8,128)}, u32[]{:S(2)}) copy-start(f32[1024,128]{1,0:T(8,128)} %weight_ref.1) | copy-start | bytes 1572868
  74.9 15.1 %all-to-all-start.3 = ((bf16[64,8,128]{2,1,0:T(8,128)(2,1)}), bf16[64,8,128]{2,1,0:T(8,128)(2,1)S(1)}, u32[]{:S(2)}, u32[]{:S(2)}) async-start(bf16[64,8,128]{2,1,0:T(8,128)(2,1)} %shard_map.125), calls=%async_computation.3 | async-start | bytes 262144 | tf_op jit(solution)/shard_map/all_to_all | solution.py:277
  80.3 9.8 %copy-start.9 = (f32[128]{0:T(128)S(1)}, f32[128]{0:T(128)}, u32[]{:S(2)}) copy-start(f32[128]{0:T(128)} %param.21) | copy-start | bytes 1540

commit v3 on v2

v3 whole, which is shorter than its diff:
```python
import math

import jax
import jax.numpy as jnp
from jax import lax
from jax.experimental import pallas as pl
from jax.experimental.pallas import tpu as pltpu
from jax.sharding import PartitionSpec as P

BF = jnp.bfloat16
F32 = jnp.float32
VMEM = pl.BlockSpec(memory_space=pltpu.VMEM)
SMEM = pl.BlockSpec(memory_space=pltpu.SMEM)
HBM = pl.BlockSpec(memory_space=pltpu.HBM)


def dot(a, b):
    return jnp.dot(a, b, preferred_element_type=F32)


def dot_nt(a, b):
    return lax.dot_general(a, b, (((1,), (1,)), ((), ())), preferred_element_type=F32)


def dot_tn(a, b):
    return lax.dot_general(a, b, (((0,), (0,)), ((), ())), preferred_element_type=F32)


def dot_split(x, matrix):
    high = x.astype(BF)
    low = (x - high.astype(F32)).astype(BF)
    return dot(high, matrix) + dot(low, matrix)


def iota(shape, dim):
    return lax.broadcasted_iota(jnp.int32, shape, dim)


def norm_groups(x):
    matrix = jnp.where(iota((128, 128), 0) // 64 == iota((128, 128), 1) // 64, 1.0 / 64, 0.0)
    matrix = matrix.astype(BF)
    centred = x - dot_split(x, matrix)
    spread = dot_split(centred * centred, matrix)
    return centred * lax.rsqrt(spread + 1e-05)


def both_halves(x, odd):
    turned = pltpu.roll(x, 64, axis=1)
    low = iota(x.shape, 1) < 64
    return jnp.where(low, turned, x) if odd else jnp.where(low, x, turned)


def send_kernel(rows_hbm, pair_hbm, weight_hbm, out_ref, rows_ref, pair_ref, weight_ref, sems):
    copies = [pltpu.make_async_copy(rows_hbm, rows_ref, sems.at[0]),
              pltpu.make_async_copy(pair_hbm, pair_ref, sems.at[1]),
              pltpu.make_async_copy(weight_hbm, weight_ref, sems.at[2])]
    for copy in copies:
        copy.start()
    for copy in copies[1:]:
        copy.wait()
    pair = pair_ref[...].astype(F32)
    pair = pair - jnp.mean(pair, axis=-1, keepdims=True)
    pair = pair * lax.rsqrt(jnp.mean(pair * pair, axis=-1, keepdims=True) + 1e-05)
    lane = iota((8, 128), 1)
    terms = jnp.zeros((8, 128), F32)
    for h in range(8):
        bias = jnp.sum(pair * weight_ref[h:h + 1, :], axis=-1, keepdims=True)
        for k in range(3):
            term = bias.astype(BF).astype(F32)
            bias = bias - term
            terms = jnp.where(lane == k * 8 + h, term, terms)
    terms = terms.astype(BF)
    for peer in range(8):
        out_ref[peer, 4] = terms
    copies[0].wait()
    for peer in range(8):
        low = rows_ref[peer * 8:peer * 8 + 4].astype(F32)
        high = rows_ref[peer * 8 + 4:peer * 8 + 8].astype(F32)
        out_ref[peer, 0:4] = jnp.concatenate([low, high], axis=-1).astype(BF)


def bias_kernel(count_ref, mask_ref, members_ref, all_ref, out_ref, scratch):
    terms = all_ref[:, 4].astype(F32).reshape(64, 128).T
    bias = terms[0:8] + terms[8:16] + terms[16:24]
    bias = bias + jnp.where(mask_ref[lax.axis_index("seq")] == 1, 0.0, -1000000.0)
    scratch[...] = jnp.concatenate([bias, bias], axis=1)
    for k in range(4):
        row = jnp.where(iota((1, 128), 1) < 64, scratch[2 * k:2 * k + 1, :],
                        scratch[2 * k + 1:2 * k + 2, :])
        out_ref[:, :, k * 128:(k + 1) * 128] = jnp.broadcast_to(row[None], (64, 1, 128))
    weight = jnp.where(iota((1, 64), 1) < count_ref[0], members_ref[...], 0).astype(F32)
    total = jnp.sum(weight, axis=1, keepdims=True)
    out_ref[:, :, 512:640] = jnp.broadcast_to(total[None], (64, 1, 128))


def project_kernel(all_ref, in_w_ref, outer_w_ref, raw_out, k_out, q_out, v_out, gate_out, w_out):
    raw = jnp.concatenate([all_ref[:, p].astype(F32).reshape(64, 128) for p in range(4)], axis=0)
    normed = norm_groups(raw).astype(BF)
    raw = raw.astype(BF)
    weight = in_w_ref[...]
    turned = weight.astype(F32).T
    turned = jnp.concatenate([turned[0:64], turned[128:256]], axis=0)
    zero = jnp.zeros_like(turned)
    key_w = weight[:, 64:128]
    key_zero = jnp.zeros_like(key_w)
    row, lane = iota((64, 128), 0), iota((64, 128), 1)
    for half in range(2):
        sides = [turned, zero] if half == 0 else [zero, turned]
        qvg = dot_nt(jnp.concatenate(sides, axis=1).astype(BF), normed)
        sides = [key_w, key_zero] if half == 0 else [key_zero, key_w]
        k_out[half] = dot(normed, jnp.concatenate(sides, axis=0)).astype(BF)
        pick = (lane == row + 64 * half).astype(BF)
        raw_out[:, half * 256:(half + 1) * 256] = dot_nt(pick, raw)
        gate_out[:, half * 256:(half + 1) * 256] = jax.nn.sigmoid(qvg[128:192])
        for place in range(4):
            e = half * 4 + place
            v_out[e] = qvg[64:128, place * 64:(place + 1) * 64].astype(BF)
            q = qvg[0:64, place // 2 * 128:(place // 2 + 1) * 128] * (1.0 / math.sqrt(8))
            q = both_halves(q, place % 2)
            for k in range(4):
                own = row // 8 == 2 * k + lane // 64
                q_out[e, :, k * 128:(k + 1) * 128] = jnp.where(own, q, 0.0).astype(BF)
    for c in range(32):
        w_out[c % 2, :, c // 2 * 32:(c // 2 + 1) * 32] = (
            outer_w_ref[c * 32:(c + 1) * 32, :].T.astype(BF))


def attend_kernel(count_ref, members_ref, mask_ref, bias_ref, raw_ref, k_ref, q_ref, v_ref,
                  gate_ref, out_w_ref, factor_ref, out_ref, left_scr, right_scr):
    bias = jnp.concatenate([bias_ref[pl.ds(k, 64, stride=5), :] for k in range(4)], axis=1)
    lane = iota((8, 128), 1)
    probs = []
    for e in range(8):
        keys = k_ref[e // 4, e % 4 * 64:(e % 4 + 1) * 64, :]
        scores = dot(keys, q_ref[e]) + bias
        expo = jnp.exp(scores - jnp.max(scores, axis=0, keepdims=True))
        probs.append((expo * (1.0 / jnp.sum(expo, axis=0, keepdims=True))).astype(BF))
    columns = []
    for pair in range(4):
        full = [dot(v_ref[2 * pair + odd], probs[2 * pair + odd]) for odd in range(2)]
        heads = []
        for h in range(8):
            low, high = [f[h * 8:(h + 1) * 8, h // 2 * 128:(h // 2 + 1) * 128] for f in full]
            if h % 2 == 0:
                high = pltpu.roll(high, 64, axis=1)
            else:
                low = pltpu.roll(low, 64, axis=1)
            heads.append(jnp.where(lane < 64, low, high))
        columns.append(jnp.concatenate(heads, axis=0))
    context = jnp.concatenate(columns, axis=1)
    gated = (gate_ref[...] * context).astype(BF)

    base = lax.axis_index("res") * 8
    keep = (mask_ref[...] == 1).astype(F32)
    keep = jnp.concatenate([keep, keep], axis=1)
    usable = [(base + e < count_ref[0]).astype(F32) for e in range(8)]
    weights = [members_ref[base + e].astype(F32) * usable[e] for e in range(8)]
    low = iota((1, 128), 1) < 64
    used = jnp.concatenate([jnp.where(low, usable[2 * p], usable[2 * p + 1]) for p in range(4)],
                           axis=1)
    scale = jnp.concatenate([jnp.where(low, weights[2 * p], weights[2 * p + 1]) * keep
                             for p in range(4)], axis=1)

    out_w = out_w_ref[...]
    x = raw_ref[...] + dot_tn(out_w, gated).astype(BF).astype(F32) * used
    x = x - jnp.mean(x, axis=0, keepdims=True)
    x = (x * lax.rsqrt(jnp.mean(x * x, axis=0, keepdims=True) + 1e-05)).astype(BF)
    factor = factor_ref[...]

    left = dot_tn(factor[:, 0:32], x) * scale
    for e in range(8):
        both = left[:, e // 2 * 128:(e // 2 + 1) * 128]
        left_scr[e * 32:(e + 1) * 32, :] = both_halves(both, e % 2)
    for c in range(16):
        block = jnp.where(lane < 64, left_scr[pl.ds(2 * c, 8, stride=32), :],
                          left_scr[pl.ds(2 * c + 1, 8, stride=32), :]).astype(BF)
        for peer in range(8):
            out_ref[peer, c] = block

    update = dot_tn(gated, jnp.concatenate([out_w, out_w], axis=1))
    for place in range(4):
        first = jnp.where(iota((64, 128), 1) < 64,
                          update[place * 64:(place + 1) * 64] * usable[place],
                          update[(place + 4) * 64:(place + 5) * 64] * usable[place + 4])
        first = first.reshape(8, 8, 128).astype(BF)
        for peer in range(8):
            out_ref[peer, 16 + place] = first[peer]

    right_w = jnp.concatenate([factor[:, 32:64]] * 4, axis=1)
    right_scr[...] = dot_tn(x, right_w)
    for peer in range(8):
        for quad in range(2):
            first = peer * 8 + quad * 4
            a, b, c, d = [right_scr[pl.ds(first + j, 8, stride=64), :] for j in range(4)]
            block = jnp.where(lane < 64, jnp.where(lane < 32, a, b), jnp.where(lane < 96, c, d))
            out_ref[peer, 20 + quad] = block.astype(BF)


def outer_kernel(mask_ref, all_ref, weight_ref, out_ref, part_scr):
    def gathered(block):
        return all_ref[:, block].astype(F32).reshape(64, 128)

    base = lax.axis_index("res") * 8
    lane = iota((1, 128), 1)
    right = []
    for quad in range(2):
        keep = jnp.zeros((1, 128), F32)
        for j in range(4):
            mine = (mask_ref[base + quad * 4 + j] == 1).astype(F32)
            keep = jnp.where(lane // 32 == j, mine, keep)
        right.append((gathered(20 + quad) * keep).astype(BF))
    right = jnp.concatenate(right, axis=1)
    left = jnp.concatenate([gathered(c).astype(BF) for c in range(16)], axis=1)
    outer = dot_tn(right, left).astype(BF)
    pick = (iota((64, 128), 0) == iota((64, 128), 1)).astype(BF)
    for j in range(8):
        rows = outer[j * 32:(j + 1) * 32]
        stacked = jnp.concatenate([rows[:, c * 128:(c + 1) * 128] for c in range(16)], axis=0)
        even, odd = dot(weight_ref[0], stacked), dot(weight_ref[1], stacked)
        part = (even + pltpu.roll(odd, 64, axis=1)).astype(BF)
        part_scr[pl.ds(j, 64, stride=8), :] = dot_nt(pick, part)
    out_ref[...] = part_scr[...].reshape(64, 8, 128).astype(BF)


def update_kernel(all_ref, out_ref):
    for place in range(4):
        block = all_ref[:, 16 + place].astype(F32)
        for half in range(2):
            part = block[:, :, half * 64:(half + 1) * 64].astype(BF)
            for peer in range(8):
                out_ref[peer * 8 + half * 4 + place] = part[peer]


def call(kernel, outs, specs, scratch=(), flops=0, limit=8):
    return pl.pallas_call(
        kernel,
        out_shape=[jax.ShapeDtypeStruct(shape, kind) for shape, kind in outs],
        in_specs=specs,
        out_specs=[VMEM] * len(outs),
        scratch_shapes=[s if not isinstance(s, tuple) else pltpu.VMEM(*s) for s in scratch],
        cost_estimate=pl.CostEstimate(flops=flops, bytes_accessed=1 << 20, transcendentals=0),
        compiler_params=pltpu.CompilerParams(vmem_limit_bytes=limit << 20),
    )


def local(
    alignment_rows,
    pair_features,
    sequence_block_count,
    cluster_member_count,
    residue_present_mask,
    attention_in_weight,
    attention_out_weight,
    pair_bias_weight,
    outer_factor_weight,
    outer_output_weight,
    outer_product_bias,
):
    (send,) = call(
        send_kernel, [((8, 5, 8, 128), BF)], [HBM] * 3,
        [((64, 8, 64), BF), ((8, 128), BF), ((8, 128), F32), pltpu.SemaphoreType.DMA((3,))],
    )(alignment_rows, pair_features.reshape(8, 128), pair_bias_weight.T)
    rows_all = lax.all_to_all(send, "res", split_axis=0, concat_axis=0, tiled=True)
    (bias_send,) = call(
        bias_kernel, [((64, 1, 640), F32)], [SMEM] * 2 + [VMEM] * 2, [((8, 128), F32)],
    )(sequence_block_count, residue_present_mask, cluster_member_count.reshape(1, 64), rows_all)
    bias_all = lax.all_to_all(bias_send, "seq", split_axis=0, concat_axis=0, tiled=True)
    bias_all = bias_all.reshape(320, 128)
    raw, keys, queries, values, gate, outer_w = call(
        project_kernel,
        [((64, 512), F32), ((2, 256, 64), BF), ((8, 64, 512), BF), ((8, 64, 64), BF),
         ((64, 512), F32), ((2, 128, 512), BF)],
        [VMEM] * 3,
        flops=1 << 30,
    )(rows_all, attention_in_weight, outer_output_weight)
    (factor_send,) = call(
        attend_kernel, [((8, 22, 8, 128), BF)], [SMEM] * 2 + [VMEM] * 9,
        [((256, 128), F32), ((512, 128), F32)],
    )(sequence_block_count, cluster_member_count, residue_present_mask.reshape(1, 64), bias_all,
      raw, keys, queries, values, gate, attention_out_weight, outer_factor_weight)
    factor_all = lax.all_to_all(factor_send, "res", split_axis=0, concat_axis=0, tiled=True)
    (partial,) = call(
        outer_kernel, [((64, 8, 128), BF)], [SMEM] + [VMEM] * 2, [((512, 128), F32)],
    )(residue_present_mask, factor_all, outer_w)
    arrived = lax.all_to_all(partial, "seq", split_axis=0, concat_axis=0, tiled=True)
    (row_attention_update,) = call(
        update_kernel, [((64, 8, 64), BF)], [VMEM], flops=1 << 30,
    )(factor_all)
    summed = arrived.astype(F32).sum(axis=0)
    weight_sum = jnp.sum(bias_all.reshape(64, 640)[:, 512])
    pair_update = (summed / weight_sum + outer_product_bias).astype(BF)
    return (row_attention_update, pair_update[None])


def solution(mesh):
    return jax.shard_map(
        local,
        mesh=mesh,
        in_specs=(
            P("seq", "res", None),
            P("res", "seq", None),
            P("seq"),
            P("seq"),
            P(),
            P(),
            P(),
            P(),
            P(),
            P(),
            P(),
        ),
        out_specs=(P("seq", "res", None), P("seq", "res", None)),
        check_vma=False,
    )
```

time: 91.8 us -> 86.7 us (0.944)
  blocking collectives: 38.7 us -> 16.8 us
  starting transfers between devices: 11.6 us -> 28.5 us
  waiting for transfers between devices: 27.3 us -> 24.8 us
  Pallas kernels: 8.77 us -> 10.4 us
    all_to_all x2 -> x1, blocking collectives: 38.7 us -> 16.8 us  [local(): lax.all_to_all(factor_send, 'res', split_axis=0, concat_axis=0, tiled=True)]
    all_to_all x1 -> x2, starting transfers between devices: 6.95 us -> 23.2 us  [the longest x1 15.6 us: local(): lax.all_to_all(bias_send, 'seq', split_axis=0, concat_axis=0, tiled=True)]
    all_to_all x1 -> x2, waiting for transfers between devices: 17.6 us -> 15.9 us  [the longest x1 9.21 us: local(): lax.all_to_all(bias_send, 'seq', split_axis=0, concat_axis=0, tiled=True)]
    pallas_call x4 -> x6, Pallas kernels: 8.77 us -> 10.4 us  [the longest x1 3.67 us: local(): call(outer_kernel, [((64, 8, 128), BF)], [SMEM] + [VMEM] * 2, [((512, 128...]
    unnamed x20 -> x21, local copies, waits for them, and re-layouts: 1.58 us -> 2.32 us
  transfers between devices with their start and end apart: 2 -> 3, of which waited for: 2 -> 3; matrix products, arithmetic and copies ran while one was open for 1% -> 1% of each run, Pallas kernels for 0% -> 2%
where the time goes in v3:
time: 86.7 us; the launch traced here: 86.3 us
  starting transfers between devices  28.5 us (33%)
  waiting for transfers between devices  24.8 us (29%)
  blocking collectives  16.8 us (19%)
  Pallas kernels  10.4 us (12%)
  local copies, waits for them, and re-layouts  2.32 us (3%)
  other arithmetic  2.03 us (2%)
  between operations  1.4 us (2%)
    all_to_all x1, blocking collectives, local(): lax.all_to_all(factor_send, 'res', split_axis=0, concat_axis=0, tiled=True)  16.8 us
    all_to_all x1, starting transfers between devices, local(): lax.all_to_all(bias_send, 'seq', split_axis=0, concat_axis=0, tiled=True)  15.6 us
    all_to_all x1, waiting for transfers between devices, local(): lax.all_to_all(bias_send, 'seq', split_axis=0, concat_axis=0, tiled=True)  9.21 us
    all_to_all x1, waiting for transfers between devices, local(): lax.all_to_all(partial, 'seq', split_axis=0, concat_axis=0, tiled=True)  8.87 us
    all_to_all x1, starting transfers between devices, local(): lax.all_to_all(send, 'res', split_axis=0, concat_axis=0, tiled=True)  7.65 us
    all_to_all x1, waiting for transfers between devices, local(): lax.all_to_all(send, 'res', split_axis=0, concat_axis=0, tiled=True)  6.72 us
    all_to_all x1, starting transfers between devices, local(): lax.all_to_all(partial, 'seq', split_axis=0, concat_axis=0, tiled=True)  5.32 us
    pallas_call x1, Pallas kernels, local(): call(outer_kernel, [((64, 8, 128), BF)], [SMEM] + [VMEM] * 2, [((512, 128...  3.67 us
  transfers between devices with their start and end apart: 3, of which 3 were waited for; matrix products, arithmetic and copies ran while one was open for 1% of the time, Pallas kernels for 2%

profile of v3, /device:TPU:1, one launch (start us, length us, event | category | flops | bytes accessed | tf_op | source)
XLA Modules:
  0.0 86.3 jit_solution(8616655791747932217)
XLA Ops:
  0.6 0.0 copy-start.6
  0.6 0.7 copy-done.6
  1.3 0.0 copy-start
  1.3 0.9 %copy-done = bf16[64,8,64]{2,1,0:T(8,128)(2,1)S(1)} copy-done((bf16[64,8,64]{2,1,0:T(8,128)(2,1)S(1)}, bf16[64,8,64]{2,1,0:T(8,128)(2,1)}, u32[]{:S(2)}) %copy-start) | copy-done | bytes 65560
  2.2 0.0 copy-start.4
  2.2 0.7 copy-done.4
  2.9 1.2 %shard_map.122 = bf16[8,5,8,128]{3,2,1,0:T(8,128)(2,1)} custom-call(bf16[64,8,64]{2,1,0:T(8,128)(2,1)S(1)} %copy-done, bf16[8,128]{1,0:T(8,128)(2,1)S(1)} %bitcast.16, f32[8,128]{1,0:T(8,128)S(1)} %bitcast.14), custom_call_target="tpu_custom_call" | custom-call | bytes 1048576 | tf_op jit(solution)/shard_map/pallas_call | solution.py:259
  4.1 7.7 %all-to-all-start = ((bf16[8,5,8,128]{3,2,1,0:T(8,128)(2,1)}), bf16[8,5,8,128]{3,2,1,0:T(8,128)(2,1)S(1)}, u32[]{:S(2)}, u32[]{:S(2)}) async-start(bf16[8,5,8,128]{3,2,1,0:T(8,128)(2,1)} %shard_map.122), calls=%async_computation | async-start | bytes 163840 | tf_op jit(solution)/shard_map/all_to_all | solution.py:263
  12.4 0.0 copy-start.3
  12.4 0.0 copy-start.5
  12.4 0.0 copy-start.7
  12.4 6.7 %all-to-all-done.all_ref = bf16[8,5,8,128]{3,2,1,0:T(8,128)(2,1)S(1)} async-done(((bf16[8,5,8,128]{3,2,1,0:T(8,128)(2,1)}), bf16[8,5,8,128]{3,2,1,0:T(8,128)(2,1)S(1)}, u32[]{:S(2)}, u32[]{:S(2)}) %all-to-all-start) | async-done | bytes 81952 | tf_op jit(solution)/shard_map/all_to_all | solution.py:263
  19.1 0.0 copy-done.3
  19.1 0.0 copy-done.5
  19.1 1.4 %shard_map.123 = f32[64,1,640]{2,1,0:T(1,128)} custom-call(s32[1]{0:T(128)S(6)} %copy.16.count_ref, s32[64]{0:T(128)S(1)} %copy-done.3, s32[1,64]{1,0:T(1,128)S(1)} %bitcast.15, bf16[8,5,8,128]{3,2,1,0:T(8,128)(2,1)S(1)} %all-to-all-done.all_ref), custom_call_target="tpu_custom_call" | custom-call | bytes 1048576 | tf_op jit(solution)/shard_map/pallas_call | solution.py:264
  20.6 0.0 copy-start.8
  20.6 15.6 %all-to-all-start.1 = ((f32[64,1,640]{2,1,0:T(1,128)}), f32[64,1,640]{2,1,0:T(1,128)S(1)}, u32[]{:S(2)}, u32[]{:S(2)}) async-start(f32[64,1,640]{2,1,0:T(1,128)} %shard_map.123), calls=%async_computation.1 | async-start | bytes 327680 | tf_op jit(solution)/shard_map/all_to_all | solution.py:267
  36.1 0.0 copy-done.7
  36.2 0.0 copy-done.8
  36.2 0.0 copy-start.1
  36.2 0.0 copy-start.2
  36.2 1.3 %shard_map.124 = (f32[64,512]{1,0:T(8,128)S(1)}, bf16[2,256,64]{2,1,0:T(8,128)(2,1)S(1)}, bf16[8,64,512]{2,1,0:T(8,128)(2,1)S(1)}, bf16[8,64,64]{2,1,0:T(8,128)(...) custom-call(bf16[8,5,8,128]{3,2,1,0:T(8,128)(2,1)S(1)} %all-to-all-done.all_ref, ...), custom_call_target="tpu_custom_call" | custom-call | flops 1073741824 | bytes 1048576 | tf_op jit(solution)/shard_map/pallas_call | solution.py:269
  37.5 9.2 %all-to-all-done.1 = f32[64,1,640]{2,1,0:T(1,128)S(1)} async-done(((f32[64,1,640]{2,1,0:T(1,128)}), f32[64,1,640]{2,1,0:T(1,128)S(1)}, u32[]{:S(2)}, u32[]{:S(2)}) %all-to-all-start.1) | async-done | bytes 163872 | tf_op jit(solution)/shard_map/all_to_all | solution.py:267
  46.7 0.0 copy-done.1
  46.7 0.0 copy-done.2
  46.7 2.0 %shard_map.125 = bf16[8,22,8,128]{3,2,1,0:T(8,128)(2,1)S(1)} custom-call(s32[1]{0:T(128)S(6)} %copy.16.count_ref, s32[64]{0:T(128)S(1)} %copy-done.5, s32[1,64]{1,0:T(1,128)S(1)} %bitcast.13, f32[320,128]{1,0:T(8,128)S(1)} %bitcast.12, f32[64,512]{1,0:T(8,128)S(1)} %get-tuple-element.8.raw_ref, bf16[2,256,64]{2,1,0:T(8,128)(2,1)S(1)} %get-tuple-element.9.k_ref, ...), custom_call_target="tpu_custom_call" | custom-call | bytes 1048576 | tf_op jit(solution)/shard_map/pallas_call | solution.py:276
  48.8 16.8 %all_to_all.20.all_ref = bf16[8,22,8,128]{3,2,1,0:T(8,128)(2,1)S(1)} all-to-all(bf16[8,22,8,128]{3,2,1,0:T(8,128)(2,1)S(1)} %shard_map.125), channel_id=1, replica_groups=mesh['seq'=64,'res'=8] {'res'}, dimensions={0} | all-to-all | bytes 720896 | tf_op jit(solution)/shard_map/all_to_all | solution.py:281
  65.6 3.7 %shard_map.127 = bf16[64,8,128]{2,1,0:T(8,128)(2,1)} custom-call(s32[64]{0:T(128)S(1)} %copy-done.3, bf16[8,22,8,128]{3,2,1,0:T(8,128)(2,1)S(1)} %all_to_all.20.all_ref, bf16[2,128,512]{2,1,0:T(8,128)(2,1)S(1)} %get-tuple-element.13.weight_ref), custom_call_target="tpu_custom_call" | custom-call | bytes 1048576 | tf_op jit(solution)/shard_map/pallas_call | solution.py:282
  69.2 5.3 %all-to-all-start.3 = ((bf16[64,8,128]{2,1,0:T(8,128)(2,1)}), bf16[64,8,128]{2,1,0:T(8,128)(2,1)S(1)}, u32[]{:S(2)}, u32[]{:S(2)}) async-start(bf16[64,8,128]{2,1,0:T(8,128)(2,1)} %shard_map.127), calls=%async_computation.3 | async-start | bytes 262144 | tf_op jit(solution)/shard_map/all_to_all | solution.py:285
  74.6 0.7 slice_reduce_fusion
  75.3 0.8 shard_map.126
  76.0 0.0 copy-start.9
  76.0 8.9 %all-to-all-done.3 = bf16[64,8,128]{2,1,0:T(8,128)(2,1)S(1)} async-done(((bf16[64,8,128]{2,1,0:T(8,128)(2,1)}), bf16[64,8,128]{2,1,0:T(8,128)(2,1)S(1)}, u32[]{:S(2)}, u32[]{:S(2)}) %all-to-all-start.3) | async-done | bytes 131104 | tf_op jit(solution)/shard_map/all_to_all | solution.py:285
  84.9 0.1 convert_reduce_fusion
  85.0 0.0 copy-done.9
  85.0 1.3 %fusion = bf16[1,8,128]{2,1,0:T(8,128)(2,1)} fusion(f32[8,128]{1,0:T(8,128)S(1)} %convert_reduce_fusion, f32[128]{0:T(128)S(1)} %copy-done.9, f32[]{:T(128)} %slice_reduce_fusion), kind=kLoop, calls=%fused_computation.4 | loop fusion | flops 3072 | bytes 6660 | tf_op jit(solution)/shard_map/convert_element_type | solution.py:291
  (1 shorter events, 0.0 us)
Async XLA Ops:
  0.6 0.7 copy-start.6
  1.3 0.9 %copy-start = (bf16[64,8,64]{2,1,0:T(8,128)(2,1)S(1)}, bf16[64,8,64]{2,1,0:T(8,128)(2,1)}, u32[]{:S(2)}) copy-start(bf16[64,8,64]{2,1,0:T(8,128)(2,1)} %rows_hbm.1) | copy-start | bytes 196612
  2.2 0.7 copy-start.4
  4.1 15.1 %all-to-all-start = ((bf16[8,5,8,128]{3,2,1,0:T(8,128)(2,1)}), bf16[8,5,8,128]{3,2,1,0:T(8,128)(2,1)S(1)}, u32[]{:S(2)}, u32[]{:S(2)}) async-start(bf16[8,5,8,128]{3,2,1,0:T(8,128)(2,1)} %shard_map.122), calls=%async_computation | async-start | bytes 163840 | tf_op jit(solution)/shard_map/all_to_all | solution.py:263
  12.4 6.8 %copy-start.3 = (s32[64]{0:T(128)S(1)}, s32[64]{0:T(128)}, u32[]{:S(2)}) copy-start(s32[64]{0:T(128)} %mask_ref.3) | copy-start | bytes 772
  12.4 6.7 %copy-start.5 = (s32[64]{0:T(128)S(1)}, s32[64]{0:T(128)}, u32[]{:S(2)}) copy-start(s32[64]{0:T(128)} %members_ref.1) | copy-start | bytes 772
  12.4 23.7 %copy-start.7 = (f32[1024,128]{1,0:T(8,128)S(1)}, f32[1024,128]{1,0:T(8,128)}, u32[]{:S(2)}) copy-start(f32[1024,128]{1,0:T(8,128)} %outer_w_ref.1) | copy-start | bytes 1572868
  20.6 15.6 %copy-start.8 = (bf16[64,256]{1,0:T(8,128)(2,1)S(1)}, bf16[64,256]{1,0:T(8,128)(2,1)}, u32[]{:S(2)}) copy-start(bf16[64,256]{1,0:T(8,128)(2,1)} %in_w_ref.1) | copy-start | bytes 98308
  20.6 26.2 %all-to-all-start.1 = ((f32[64,1,640]{2,1,0:T(1,128)}), f32[64,1,640]{2,1,0:T(1,128)S(1)}, u32[]{:S(2)}, u32[]{:S(2)}) async-start(f32[64,1,640]{2,1,0:T(1,128)} %shard_map.123), calls=%async_computation.1 | async-start | bytes 327680 | tf_op jit(solution)/shard_map/all_to_all | solution.py:267
  36.2 10.6 %copy-start.1 = (bf16[64,64]{1,0:T(8,128)(2,1)S(1)}, bf16[64,64]{1,0:T(8,128)(2,1)}, u32[]{:S(2)}) copy-start(bf16[64,64]{1,0:T(8,128)(2,1)} %out_w_ref.1) | copy-start | bytes 24580
  36.2 10.6 %copy-start.2 = (bf16[64,64]{1,0:T(8,128)(2,1)S(1)}, bf16[64,64]{1,0:T(8,128)(2,1)}, u32[]{:S(2)}) copy-start(bf16[64,64]{1,0:T(8,128)(2,1)} %factor_ref.1) | copy-start | bytes 24580
  69.2 15.7 %all-to-all-start.3 = ((bf16[64,8,128]{2,1,0:T(8,128)(2,1)}), bf16[64,8,128]{2,1,0:T(8,128)(2,1)S(1)}, u32[]{:S(2)}, u32[]{:S(2)}) async-start(bf16[64,8,128]{2,1,0:T(8,128)(2,1)} %shard_map.127), calls=%async_computation.3 | async-start | bytes 262144 | tf_op jit(solution)/shard_map/all_to_all | solution.py:285
  76.0 8.9 %copy-start.9 = (f32[128]{0:T(128)S(1)}, f32[128]{0:T(128)}, u32[]{:S(2)}) copy-start(f32[128]{0:T(128)} %param.21) | copy-start | bytes 1540

commit v4 on v3

--- a/solution.py
+++ b/solution.py
@@ -50,50 +50,59 @@
     return jnp.where(low, turned, x) if odd else jnp.where(low, x, turned)
 
 
-def send_kernel(rows_hbm, pair_hbm, weight_hbm, out_ref, rows_ref, pair_ref, weight_ref, sems):
-    copies = [pltpu.make_async_copy(rows_hbm, rows_ref, sems.at[0]),
-              pltpu.make_async_copy(pair_hbm, pair_ref, sems.at[1]),
-              pltpu.make_async_copy(weight_hbm, weight_ref, sems.at[2])]
+def bias_kernel(pair_hbm, weight_hbm, members_hbm, count_hbm, out_ref,
+                pair_ref, weight_ref, members_ref, count_ref, sems):
+    copies = [pltpu.make_async_copy(pair_hbm, pair_ref, sems.at[0]),
+              pltpu.make_async_copy(weight_hbm, weight_ref, sems.at[1]),
+              pltpu.make_async_copy(members_hbm, members_ref, sems.at[2]),
+              pltpu.make_async_copy(count_hbm, count_ref, sems.at[3])]
     for copy in copies:
         copy.start()
-    for copy in copies[1:]:
+    for copy in copies:
         copy.wait()
     pair = pair_ref[...].astype(F32)
     pair = pair - jnp.mean(pair, axis=-1, keepdims=True)
     pair = pair * lax.rsqrt(jnp.mean(pair * pair, axis=-1, keepdims=True) + 1e-05)
-    lane = iota((8, 128), 1)
-    terms = jnp.zeros((8, 128), F32)
+    row, lane = iota((8, 128), 0), iota((8, 128), 1)
+    bias = jnp.zeros((8, 128), F32)
     for h in range(8):
-        bias = jnp.sum(pair * weight_ref[h:h + 1, :], axis=-1, keepdims=True)
-        for k in range(3):
-            term = bias.astype(BF).astype(F32)
-            bias = bias - term
-            terms = jnp.where(lane == k * 8 + h, term, terms)
-    terms = terms.astype(BF)
-    for peer in range(8):
-        out_ref[peer, 4] = terms
-    copies[0].wait()
+        column = jnp.sum(pair * weight_ref[h:h + 1, :], axis=-1, keepdims=True)
+        bias = jnp.where(lane == h * 8 + row, column, bias)
+    bias = jnp.sum(bias, axis=0, keepdims=True)
+    weight = jnp.where(iota((1, 64), 1) < count_ref[...], members_ref[...], 0).astype(F32)
+    bias = jnp.where(lane[0:1] < 64, bias, jnp.sum(weight, axis=1, keepdims=True))
+    out_ref[...] = jnp.broadcast_to(bias[None], (64, 1, 128))
+
+
+def pack_kernel(rows_ref, out_ref):
     for peer in range(8):
         low = rows_ref[peer * 8:peer * 8 + 4].astype(F32)
         high = rows_ref[peer * 8 + 4:peer * 8 + 8].astype(F32)
-        out_ref[peer, 0:4] = jnp.concatenate([low, high], axis=-1).astype(BF)
-
-
-def bias_kernel(count_ref, mask_ref, members_ref, all_ref, out_ref, scratch):
-    terms = all_ref[:, 4].astype(F32).reshape(64, 128).T
-    bias = terms[0:8] + terms[8:16] + terms[16:24]
-    bias = bias + jnp.where(mask_ref[lax.axis_index("seq")] == 1, 0.0, -1000000.0)
-    scratch[...] = jnp.concatenate([bias, bias], axis=1)
-    for k in range(4):
-        row = jnp.where(iota((1, 128), 1) < 64, scratch[2 * k:2 * k + 1, :],
-                        scratch[2 * k + 1:2 * k + 2, :])
-        out_ref[:, :, k * 128:(k + 1) * 128] = jnp.broadcast_to(row[None], (64, 1, 128))
-    weight = jnp.where(iota((1, 64), 1) < count_ref[0], members_ref[...], 0).astype(F32)
-    total = jnp.sum(weight, axis=1, keepdims=True)
-    out_ref[:, :, 512:640] = jnp.broadcast_to(total[None], (64, 1, 128))
-
-
-def project_kernel(all_ref, in_w_ref, outer_w_ref, raw_out, k_out, q_out, v_out, gate_out, w_out):
+        out_ref[peer] = jnp.concatenate([low, high], axis=-1).astype(BF)
+
+
+def send_kernel(rows_ref, bias_ref, out_ref):
+    for peer in range(8):
+        out_ref[peer, 0:4] = rows_ref[peer]
+    bias = bias_ref[...]
+    high = bias.astype(BF).astype(F32)
+    terms = jnp.where(iota((64, 128), 1) < 64, high, pltpu.roll(bias - high, 64, axis=1))
+    terms = terms.reshape(8, 8, 128).astype(BF)
+    for peer in range(8):
+        out_ref[peer, 4:12] = terms
+
+
+def weight_kernel(outer_w_ref, w_out, place_out):
+    for c in range(32):
+        w_out[c % 2, :, c // 2 * 32:(c // 2 + 1) * 32] = (
+            outer_w_ref[c * 32:(c + 1) * 32, :].T.astype(BF))
+    for peer in range(8):
+        row, lane = iota((128, 512), 0), iota((128, 512), 1)
+        target = row % 64 // 8 * 64 + peer * 8 + row % 8
+        place_out[peer * 128:(peer + 1) * 128, :] = (lane == target).astype(BF)
+
+
+def project(all_ref, in_w_ref, raw_out, k_out, q_out, v_out, gate_out):
     raw = jnp.concatenate([all_ref[:, p].astype(F32).reshape(64, 128) for p in range(4)], axis=0)
     normed = norm_groups(raw).astype(BF)
     raw = raw.astype(BF)
@@ -120,14 +129,17 @@
             for k in range(4):
                 own = row // 8 == 2 * k + lane // 64
                 q_out[e, :, k * 128:(k + 1) * 128] = jnp.where(own, q, 0.0).astype(BF)
-    for c in range(32):
-        w_out[c % 2, :, c // 2 * 32:(c // 2 + 1) * 32] = (
-            outer_w_ref[c * 32:(c + 1) * 32, :].T.astype(BF))
-
-
-def attend_kernel(count_ref, members_ref, mask_ref, bias_ref, raw_ref, k_ref, q_ref, v_ref,
-                  gate_ref, out_w_ref, factor_ref, out_ref, left_scr, right_scr):
-    bias = jnp.concatenate([bias_ref[pl.ds(k, 64, stride=5), :] for k in range(4)], axis=1)
+
+
+def attend_kernel(members_ref, count_ref, mask_ref, all_ref, place_ref, in_w_ref, out_w_ref,
+                  factor_ref, out_ref, raw_ref, k_ref, q_ref, v_ref, gate_ref, left_scr,
+                  right_scr):
+    project(all_ref, in_w_ref, raw_ref, k_ref, q_ref, v_ref, gate_ref)
+    terms = [all_ref[peer, 4:12].astype(F32).reshape(64, 128).astype(BF) for peer in range(8)]
+    present = jnp.where(iota((64, 64), 0) == iota((64, 64), 1), mask_ref[...], 0)
+    present = jnp.sum(present.astype(F32), axis=1, keepdims=True)
+    bias = dot(jnp.concatenate(terms, axis=1), place_ref[...])
+    bias = bias + jnp.where(present == 1.0, 0.0, -1000000.0)
     lane = iota((8, 128), 1)
     probs = []
     for e in range(8):
@@ -153,7 +165,7 @@
     base = lax.axis_index("res") * 8
     keep = (mask_ref[...] == 1).astype(F32)
     keep = jnp.concatenate([keep, keep], axis=1)
-    usable = [(base + e < count_ref[0]).astype(F32) for e in range(8)]
+    usable = [(base + e < count_ref[...]).astype(F32) for e in range(8)]
     weights = [members_ref[base + e].astype(F32) * usable[e] for e in range(8)]
     low = iota((1, 128), 1) < 64
     used = jnp.concatenate([jnp.where(low, usable[2 * p], usable[2 * p + 1]) for p in range(4)],
@@ -256,28 +268,32 @@
     outer_output_weight,
     outer_product_bias,
 ):
+    members = cluster_member_count.reshape(1, 64)
+    count = sequence_block_count.reshape(1, 1)
+    (packed,) = call(
+        pack_kernel, [((8, 4, 8, 128), BF)], [VMEM], flops=1 << 30,
+    )(alignment_rows)
+    (bias_send,) = call(
+        bias_kernel, [((64, 1, 128), F32)], [HBM] * 4,
+        [((8, 128), BF), ((8, 128), F32), ((1, 64), jnp.int32), ((1, 1), jnp.int32),
+         pltpu.SemaphoreType.DMA((4,))],
+        limit=60,
+    )(pair_features.reshape(8, 128), pair_bias_weight.T, members, count)
+    bias_all = lax.all_to_all(bias_send, "seq", split_axis=0, concat_axis=0, tiled=True)
+    bias_all = bias_all.reshape(64, 128)
+    outer_w, place = call(
+        weight_kernel, [((2, 128, 512), BF), ((1024, 512), BF)], [VMEM], flops=1 << 30,
+    )(outer_output_weight)
     (send,) = call(
-        send_kernel, [((8, 5, 8, 128), BF)], [HBM] * 3,
-        [((64, 8, 64), BF), ((8, 128), BF), ((8, 128), F32), pltpu.SemaphoreType.DMA((3,))],
-    )(alignment_rows, pair_features.reshape(8, 128), pair_bias_weight.T)
+        send_kernel, [((8, 12, 8, 128), BF)], [VMEM] * 2,
+    )(packed, bias_all)
     rows_all = lax.all_to_all(send, "res", split_axis=0, concat_axis=0, tiled=True)
-    (bias_send,) = call(
-        bias_kernel, [((64, 1, 640), F32)], [SMEM] * 2 + [VMEM] * 2, [((8, 128), F32)],
-    )(sequence_block_count, residue_present_mask, cluster_member_count.reshape(1, 64), rows_all)
-    bias_all = lax.all_to_all(bias_send, "seq", split_axis=0, concat_axis=0, tiled=True)
-    bias_all = bias_all.reshape(320, 128)
-    raw, keys, queries, values, gate, outer_w = call(
-        project_kernel,
+    (factor_send,) = call(
+        attend_kernel, [((8, 22, 8, 128), BF)], [SMEM] + [VMEM] * 7,
         [((64, 512), F32), ((2, 256, 64), BF), ((8, 64, 512), BF), ((8, 64, 64), BF),
-         ((64, 512), F32), ((2, 128, 512), BF)],
-        [VMEM] * 3,
-        flops=1 << 30,
-    )(rows_all, attention_in_weight, outer_output_weight)
-    (factor_send,) = call(
-        attend_kernel, [((8, 22, 8, 128), BF)], [SMEM] * 2 + [VMEM] * 9,
-        [((256, 128), F32), ((512, 128), F32)],
-    )(sequence_block_count, cluster_member_count, residue_present_mask.reshape(1, 64), bias_all,
-      raw, keys, queries, values, gate, attention_out_weight, outer_factor_weight)
+         ((64, 512), F32), ((256, 128), F32), ((512, 128), F32)],
+    )(cluster_member_count, count, residue_present_mask.reshape(1, 64), rows_all, place,
+      attention_in_weight, attention_out_weight, outer_factor_weight)
     factor_all = lax.all_to_all(factor_send, "res", split_axis=0, concat_axis=0, tiled=True)
     (partial,) = call(
         outer_kernel, [((64, 8, 128), BF)], [SMEM] + [VMEM] * 2, [((512, 128), F32)],
@@ -287,7 +303,7 @@
         update_kernel, [((64, 8, 64), BF)], [VMEM], flops=1 << 30,
     )(factor_all)
     summed = arrived.astype(F32).sum(axis=0)
-    weight_sum = jnp.sum(bias_all.reshape(64, 640)[:, 512])
+    weight_sum = jnp.sum(bias_all[:, 64])
     pair_update = (summed / weight_sum + outer_product_bias).astype(BF)
     return (row_attention_update, pair_update[None])
 

time: 86.7 us -> 84.5 us (0.975)
  blocking collectives: 16.8 us -> 14 us
  starting transfers between devices: 28.5 us -> 29.4 us
    all_to_all x1, blocking collectives: 16.8 us -> 14 us  [local(): lax.all_to_all(factor_send, 'res', split_axis=0, concat_axis=0, tiled=True)]
    all_to_all x1, starting transfers between devices: 5.32 us -> 7.74 us  [local(): lax.all_to_all(partial, 'seq', split_axis=0, concat_axis=0, tiled=True)]
    all_to_all x1, waiting for transfers between devices: 6.72 us -> 7.91 us  [local(): lax.all_to_all(send, 'res', split_axis=0, concat_axis=0, tiled=True)]
    all_to_all x1, waiting for transfers between devices: 9.21 us -> 8.23 us  [local(): lax.all_to_all(bias_send, 'seq', split_axis=0, concat_axis=0, tiled=True)]
    unnamed x21 -> x16, local copies, waits for them, and re-layouts: 2.32 us -> 1.58 us
    pallas_call x4 -> x5, Pallas kernels: 5.95 us -> 6.24 us  [the longest x1 2.71 us: local(): call(attend_kernel, [((8, 22, 8, 128), BF)], [SMEM] + [VMEM] * 7, [((64,...]
where the time goes in v4:
time: 84.5 us; the launch traced here: 84 us
  starting transfers between devices  29.4 us (35%)
  waiting for transfers between devices  25.2 us (30%)
  blocking collectives  14 us (17%)
  Pallas kernels  10.7 us (13%)
  other arithmetic  1.85 us (2%)
  local copies, waits for them, and re-layouts  1.58 us (2%)
  between operations  1.39 us (2%)
    all_to_all x1, starting transfers between devices, local(): lax.all_to_all(bias_send, 'seq', split_axis=0, concat_axis=0, tiled=True)  14.8 us
    all_to_all x1, blocking collectives, local(): lax.all_to_all(factor_send, 'res', split_axis=0, concat_axis=0, tiled=True)  14 us
    all_to_all x1, waiting for transfers between devices, local(): lax.all_to_all(partial, 'seq', split_axis=0, concat_axis=0, tiled=True)  9.04 us
    all_to_all x1, waiting for transfers between devices, local(): lax.all_to_all(bias_send, 'seq', split_axis=0, concat_axis=0, tiled=True)  8.23 us
    all_to_all x1, waiting for transfers between devices, local(): lax.all_to_all(send, 'res', split_axis=0, concat_axis=0, tiled=True)  7.91 us
    all_to_all x1, starting transfers between devices, local(): lax.all_to_all(partial, 'seq', split_axis=0, concat_axis=0, tiled=True)  7.74 us
    all_to_all x1, starting transfers between devices, local(): lax.all_to_all(send, 'res', split_axis=0, concat_axis=0, tiled=True)  6.82 us
    pallas_call x1, Pallas kernels, local(): call(outer_kernel, [((64, 8, 128), BF)], [SMEM] + [VMEM] * 2, [((512, 128...  3.68 us
  transfers between devices with their start and end apart: 3, of which 3 were waited for; matrix products, arithmetic and copies ran while one was open for 1% of the time, Pallas kernels for 2%

profile of v4, /device:TPU:1, one launch (start us, length us, event | category | flops | bytes accessed | tf_op | source)
XLA Modules:
  0.0 84.0 jit_solution(9247180175026952555)
XLA Ops:
  1.3 1.6 %shard_map.123 = f32[64,1,128]{2,1,0:T(1,128)} custom-call(bf16[8,128]{1,0:T(8,128)(2,1)} %bitcast.17, f32[8,128]{1,0:T(8,128)} %bitcast.16, s32[1,64]{1,0:T(1,128)} %bitcast.14, s32[1,1]{1,0:T(1,128)} %bitcast.10.count_hbm), custom_call_target="tpu_custom_call" | custom-call | bytes 1048576 | tf_op jit(solution)/shard_map/pallas_call | solution.py:276
  2.9 14.8 %all-to-all-start = ((f32[64,1,128]{2,1,0:T(1,128)}), f32[64,1,128]{2,1,0:T(1,128)S(1)}, u32[]{:S(2)}, u32[]{:S(2)}) async-start(f32[64,1,128]{2,1,0:T(1,128)} %shard_map.123), calls=%async_computation | async-start | bytes 65536 | tf_op jit(solution)/shard_map/all_to_all | solution.py:282
  17.8 0.0 copy-start.6
  17.8 0.9 %copy-done.6 = bf16[64,8,64]{2,1,0:T(8,128)(2,1)S(1)} copy-done((bf16[64,8,64]{2,1,0:T(8,128)(2,1)S(1)}, bf16[64,8,64]{2,1,0:T(8,128)(2,1)}, u32[]{:S(2)}) %copy-start.6) | copy-done | bytes 65560
  18.7 0.1 shard_map.122.rows_ref
  18.8 0.0 copy-start.5
  18.8 8.2 %all-to-all-done = f32[64,1,128]{2,1,0:T(1,128)S(1)} async-done(((f32[64,1,128]{2,1,0:T(1,128)}), f32[64,1,128]{2,1,0:T(1,128)S(1)}, u32[]{:S(2)}, u32[]{:S(2)}) %all-to-all-start) | async-done | bytes 32800 | tf_op jit(solution)/shard_map/all_to_all | solution.py:282
  27.0 0.8 shard_map.124
  27.8 6.8 %all-to-all-start.1 = ((bf16[8,12,8,128]{3,2,1,0:T(8,128)(2,1)}), bf16[8,12,8,128]{3,2,1,0:T(8,128)(2,1)S(1)}, u32[]{:S(2)}, u32[]{:S(2)}) async-start(bf16[8,12,8,128]{3,2,1,0:T(8,128)(2,1)} %shard_map.124), calls=%async_computation.1 | async-start | bytes 393216 | tf_op jit(solution)/shard_map/all_to_all | solution.py:290
  34.6 0.0 copy-done.5
  34.6 0.0 copy-start
  34.6 0.0 copy-start.1
  34.6 0.0 copy-start.2
  34.6 1.0 %shard_map.125 = (bf16[2,128,512]{2,1,0:T(8,128)(2,1)S(1)}, bf16[1024,512]{1,0:T(8,128)(2,1)S(1)}) custom-call(f32[1024,128]{1,0:T(8,128)S(1)} %copy-done.5), custom_call_target="tpu_custom_call" | custom-call | flops 1073741824 | bytes 1048576 | tf_op jit(solution)/shard_map/pallas_call | solution.py:284
  35.7 7.9 %all-to-all-done.1.all_ref = bf16[8,12,8,128]{3,2,1,0:T(8,128)(2,1)S(1)} async-done(((bf16[8,12,8,128]{3,2,1,0:T(8,128)(2,1)}), bf16[8,12,8,128]{3,2,1,0:T(8,128)(2,1)S(1)}, u32[]{:S(2)}, u32[]{:S(2)}) %all-to-all-start.1) | async-done | bytes 196640 | tf_op jit(solution)/shard_map/all_to_all | solution.py:290
  43.6 0.0 copy-start.3
  43.6 0.0 copy-start.4
  43.6 0.0 copy-done
  43.6 0.0 copy-done.1
  43.6 0.0 copy-done.2
  43.6 0.6 copy-done.3
  44.2 0.0 copy-done.4
  44.3 2.7 %shard_map.126 = bf16[8,22,8,128]{3,2,1,0:T(8,128)(2,1)S(1)} custom-call(s32[64]{0:T(128)S(1)} %copy-done.3, s32[1,1]{1,0:T(1,128)} %bitcast.11.count_ref, s32[1,64]{1,0:T(1,128)S(1)} %bitcast.15, bf16[8,12,8,128]{3,2,1,0:T(8,128)(2,1)S(1)} %all-to-all-done.1.all_ref, bf16[1024,512]{1,0:T(8,128)(2,1)S(1)} %get-tuple-element.4.place_ref, ...), custom_call_target="tpu_custom_call" | custom-call | bytes 1048576 | tf_op jit(solution)/shard_map/pallas_call | solution.py:291
  47.0 14.0 %all_to_all.20.all_ref = bf16[8,22,8,128]{3,2,1,0:T(8,128)(2,1)S(1)} all-to-all(bf16[8,22,8,128]{3,2,1,0:T(8,128)(2,1)S(1)} %shard_map.126), channel_id=1, replica_groups=mesh['seq'=64,'res'=8] {'res'}, dimensions={0} | all-to-all | bytes 720896 | tf_op jit(solution)/shard_map/all_to_all | solution.py:297
  61.0 3.7 %shard_map.128 = bf16[64,8,128]{2,1,0:T(8,128)(2,1)} custom-call(s32[64]{0:T(128)S(1)} %copy-done.4, bf16[8,22,8,128]{3,2,1,0:T(8,128)(2,1)S(1)} %all_to_all.20.all_ref, bf16[2,128,512]{2,1,0:T(8,128)(2,1)S(1)} %get-tuple-element.5.weight_ref), custom_call_target="tpu_custom_call" | custom-call | bytes 1048576 | tf_op jit(solution)/shard_map/pallas_call | solution.py:298
  64.6 7.7 %all-to-all-start.3 = ((bf16[64,8,128]{2,1,0:T(8,128)(2,1)}), bf16[64,8,128]{2,1,0:T(8,128)(2,1)S(1)}, u32[]{:S(2)}, u32[]{:S(2)}) async-start(bf16[64,8,128]{2,1,0:T(8,128)(2,1)} %shard_map.128), calls=%async_computation.3 | async-start | bytes 262144 | tf_op jit(solution)/shard_map/all_to_all | solution.py:301
  72.4 0.6 slice_reduce_fusion
  73.0 0.8 shard_map.127
  73.8 0.0 copy-start.7
  73.8 9.0 %all-to-all-done.3 = bf16[64,8,128]{2,1,0:T(8,128)(2,1)S(1)} async-done(((bf16[64,8,128]{2,1,0:T(8,128)(2,1)}), bf16[64,8,128]{2,1,0:T(8,128)(2,1)S(1)}, u32[]{:S(2)}, u32[]{:S(2)}) %all-to-all-start.3) | async-done | bytes 131104 | tf_op jit(solution)/shard_map/all_to_all | solution.py:301
  82.8 0.1 convert_reduce_fusion
  82.9 0.0 copy-done.7
  82.9 1.1 %fusion = bf16[1,8,128]{2,1,0:T(8,128)(2,1)} fusion(f32[8,128]{1,0:T(8,128)S(1)} %convert_reduce_fusion, f32[128]{0:T(128)S(1)} %copy-done.7, f32[]{:T(128)} %slice_reduce_fusion), kind=kLoop, calls=%fused_computation.3 | loop fusion | flops 3072 | bytes 6660 | tf_op jit(solution)/shard_map/convert_element_type | solution.py:307
Async XLA Ops:
  2.9 24.1 %all-to-all-start = ((f32[64,1,128]{2,1,0:T(1,128)}), f32[64,1,128]{2,1,0:T(1,128)S(1)}, u32[]{:S(2)}, u32[]{:S(2)}) async-start(f32[64,1,128]{2,1,0:T(1,128)} %shard_map.123), calls=%async_computation | async-start | bytes 65536 | tf_op jit(solution)/shard_map/all_to_all | solution.py:282
  17.8 0.9 %copy-start.6 = (bf16[64,8,64]{2,1,0:T(8,128)(2,1)S(1)}, bf16[64,8,64]{2,1,0:T(8,128)(2,1)}, u32[]{:S(2)}) copy-start(bf16[64,8,64]{2,1,0:T(8,128)(2,1)} %rows_ref.1) | copy-start | bytes 196612
  18.8 15.8 %copy-start.5 = (f32[1024,128]{1,0:T(8,128)S(1)}, f32[1024,128]{1,0:T(8,128)}, u32[]{:S(2)}) copy-start(f32[1024,128]{1,0:T(8,128)} %outer_w_ref.1) | copy-start | bytes 1572868
  27.8 15.8 %all-to-all-start.1 = ((bf16[8,12,8,128]{3,2,1,0:T(8,128)(2,1)}), bf16[8,12,8,128]{3,2,1,0:T(8,128)(2,1)S(1)}, u32[]{:S(2)}, u32[]{:S(2)}) async-start(bf16[8,12,8,128]{3,2,1,0:T(8,128)(2,1)} %shard_map.124), calls=%async_computation.1 | async-start | bytes 393216 | tf_op jit(solution)/shard_map/all_to_all | solution.py:290
  34.6 9.0 %copy-start = (bf16[64,256]{1,0:T(8,128)(2,1)S(1)}, bf16[64,256]{1,0:T(8,128)(2,1)}, u32[]{:S(2)}) copy-start(bf16[64,256]{1,0:T(8,128)(2,1)} %in_w_ref.1) | copy-start | bytes 98308
  34.6 9.0 %copy-start.1 = (bf16[64,64]{1,0:T(8,128)(2,1)S(1)}, bf16[64,64]{1,0:T(8,128)(2,1)}, u32[]{:S(2)}) copy-start(bf16[64,64]{1,0:T(8,128)(2,1)} %out_w_ref.1) | copy-start | bytes 24580
  34.6 9.0 %copy-start.2 = (bf16[64,64]{1,0:T(8,128)(2,1)S(1)}, bf16[64,64]{1,0:T(8,128)(2,1)}, u32[]{:S(2)}) copy-start(bf16[64,64]{1,0:T(8,128)(2,1)} %factor_ref.1) | copy-start | bytes 24580
  43.6 0.7 copy-start.3
  43.6 0.7 copy-start.4
  64.6 18.2 %all-to-all-start.3 = ((bf16[64,8,128]{2,1,0:T(8,128)(2,1)}), bf16[64,8,128]{2,1,0:T(8,128)(2,1)S(1)}, u32[]{:S(2)}, u32[]{:S(2)}) async-start(bf16[64,8,128]{2,1,0:T(8,128)(2,1)} %shard_map.128), calls=%async_computation.3 | async-start | bytes 262144 | tf_op jit(solution)/shard_map/all_to_all | solution.py:301
  73.8 9.1 %copy-start.7 = (f32[128]{0:T(128)S(1)}, f32[128]{0:T(128)}, u32[]{:S(2)}) copy-start(f32[128]{0:T(128)} %param.21) | copy-start | bytes 1540

commit v5 on v4

v5 whole, which is shorter than its diff:
```python
import math

import jax
import jax.numpy as jnp
from jax import lax
from jax.experimental import pallas as pl
from jax.experimental.pallas import tpu as pltpu
from jax.sharding import PartitionSpec as P

BF = jnp.bfloat16
F32 = jnp.float32
VMEM = pl.BlockSpec(memory_space=pltpu.VMEM)
SMEM = pl.BlockSpec(memory_space=pltpu.SMEM)
HBM = pl.BlockSpec(memory_space=pltpu.HBM)


def dot(a, b):
    return jnp.dot(a, b, preferred_element_type=F32)


def dot_nt(a, b):
    return lax.dot_general(a, b, (((1,), (1,)), ((), ())), preferred_element_type=F32)


def dot_tn(a, b):
    return lax.dot_general(a, b, (((0,), (0,)), ((), ())), preferred_element_type=F32)


def dot_split(x, matrix):
    high = x.astype(BF)
    low = (x - high.astype(F32)).astype(BF)
    return dot(high, matrix) + dot(low, matrix)


def iota(shape, dim):
    return lax.broadcasted_iota(jnp.int32, shape, dim)


def norm_groups(x):
    matrix = jnp.where(iota((128, 128), 0) // 64 == iota((128, 128), 1) // 64, 1.0 / 64, 0.0)
    matrix = matrix.astype(BF)
    centred = x - dot_split(x, matrix)
    spread = dot_split(centred * centred, matrix)
    return centred * lax.rsqrt(spread + 1e-05)


def both_halves(x, odd):
    turned = pltpu.roll(x, 64, axis=1)
    low = iota(x.shape, 1) < 64
    return jnp.where(low, turned, x) if odd else jnp.where(low, x, turned)


def bias_kernel(pair_hbm, weight_hbm, members_hbm, count_hbm, out_ref,
                pair_ref, weight_ref, members_ref, count_ref, sems):
    copies = [pltpu.make_async_copy(pair_hbm, pair_ref, sems.at[0]),
              pltpu.make_async_copy(weight_hbm, weight_ref, sems.at[1]),
              pltpu.make_async_copy(members_hbm, members_ref, sems.at[2]),
              pltpu.make_async_copy(count_hbm, count_ref, sems.at[3])]
    for copy in copies:
        copy.start()
    for copy in copies:
        copy.wait()
    pair = pair_ref[...].astype(F32)
    pair = pair - jnp.mean(pair, axis=-1, keepdims=True)
    pair = pair * lax.rsqrt(jnp.mean(pair * pair, axis=-1, keepdims=True) + 1e-05)
    row, lane = iota((8, 128), 0), iota((8, 128), 1)
    bias = jnp.zeros((8, 128), F32)
    for h in range(8):
        column = jnp.sum(pair * weight_ref[h:h + 1, :], axis=-1, keepdims=True)
        bias = jnp.where(lane == h * 8 + row, column, bias)
    bias = jnp.sum(bias, axis=0, keepdims=True)
    weight = jnp.where(iota((1, 64), 1) < count_ref[0], members_ref[...], 0).astype(F32)
    bias = jnp.where(lane[0:1] < 64, bias, jnp.sum(weight, axis=1, keepdims=True))
    out_ref[...] = jnp.broadcast_to(bias[None], (64, 1, 128))


def pack_kernel(rows_ref, out_ref):
    for peer in range(8):
        low = rows_ref[peer * 8:peer * 8 + 4].astype(F32)
        high = rows_ref[peer * 8 + 4:peer * 8 + 8].astype(F32)
        out_ref[peer] = jnp.concatenate([low, high], axis=-1).astype(BF)


def send_kernel(rows_ref, bias_ref, ahead_ref, out_ref, inverse_out):
    for peer in range(8):
        out_ref[peer, 0:4] = rows_ref[peer]
    bias = bias_ref[...]
    lane = iota((64, 128), 1)
    high = bias.astype(BF).astype(F32)
    terms = jnp.where(lane < 64, high, pltpu.roll(bias - high, 64, axis=1))
    terms = terms.reshape(8, 8, 128).astype(BF)
    for peer in range(8):
        out_ref[peer, 4:12] = terms
    total = jnp.sum(bias, axis=0, keepdims=True)
    total = jnp.sum(jnp.where(lane[0:1] == 64, total, 0.0), axis=1, keepdims=True)
    inverse_out[...] = jnp.broadcast_to(1.0 / total, (8, 128))


def weight_kernel(outer_w_ref, in_w_ref, out_w_ref, factor_ref, shift_ref, members_ref, mask_ref,
                  count_ref, w_out, place_out, qvg_out, key_out, wide_out, left_out, right_out,
                  shift_out, used_out, scale_out, absent_out, keep_out):
    w_out[...] = outer_w_ref[...].astype(BF)
    for peer in range(8):
        row, lane = iota((128, 512), 0), iota((128, 512), 1)
        target = row % 64 // 8 * 64 + peer * 8 + row % 8
        place_out[peer * 128:(peer + 1) * 128, :] = (lane == target).astype(BF)
    weight = in_w_ref[...]
    turned = weight.astype(F32).T
    turned = jnp.concatenate([turned[0:64], turned[128:256]], axis=0)
    zero = jnp.zeros_like(turned)
    qvg_out[0] = jnp.concatenate([turned, zero], axis=1).astype(BF)
    qvg_out[1] = jnp.concatenate([zero, turned], axis=1).astype(BF)
    key_w = weight[:, 64:128]
    zero = jnp.zeros_like(key_w)
    key_out[0] = jnp.concatenate([key_w, zero], axis=0)
    key_out[1] = jnp.concatenate([zero, key_w], axis=0)
    out_w = out_w_ref[...]
    wide_out[...] = jnp.concatenate([out_w, out_w], axis=1)
    factor = factor_ref[...]
    left_out[...] = factor[:, 0:32]
    right_out[...] = jnp.concatenate([factor[:, 32:64]] * 4, axis=1)
    shift_out[...] = jnp.broadcast_to(shift_ref[...], (8, 128))
    base = lax.axis_index("res") * 8
    count = count_ref[...]
    members = jnp.where(iota((1, 64), 1) < count, members_ref[...], 0).astype(F32)
    present = (mask_ref[...] == 1).astype(F32)
    mine = (iota((64, 512), 0) == base + iota((64, 512), 1) // 64).astype(BF)
    scale = dot(members.astype(BF), mine)
    scale_out[...] = scale * jnp.concatenate([present] * 8, axis=1)
    used_out[...] = (base + iota((1, 512), 1) // 64 < count).astype(F32)
    mine = (iota((64, 256), 0) == base + iota((64, 256), 1) // 32).astype(BF)
    keep_out[...] = dot(present.astype(BF), mine)
    column = jnp.where(iota((64, 64), 0) == iota((64, 64), 1), present, 0.0)
    column = jnp.sum(column, axis=1, keepdims=True)
    absent_out[...] = jnp.broadcast_to(jnp.where(column == 1.0, 0.0, -1000000.0), (64, 128))


def project(all_ref, qvg_ref, key_ref, raw_out, k_out, q_out, v_out, gate_out):
    raw = jnp.concatenate([all_ref[:, p].astype(F32).reshape(64, 128) for p in range(4)], axis=0)
    normed = norm_groups(raw).astype(BF)
    raw = raw.astype(BF)
    row, lane = iota((64, 128), 0), iota((64, 128), 1)
    for half in range(2):
        qvg = dot_nt(qvg_ref[half], normed)
        k_out[half] = dot(normed, key_ref[half]).astype(BF)
        pick = (lane == row + 64 * half).astype(BF)
        raw_out[:, half * 256:(half + 1) * 256] = dot_nt(pick, raw)
        gate_out[:, half * 256:(half + 1) * 256] = jax.nn.sigmoid(qvg[128:192])
        for place in range(4):
            e = half * 4 + place
            v_out[e] = qvg[64:128, place * 64:(place + 1) * 64].astype(BF)
            q = qvg[0:64, place // 2 * 128:(place // 2 + 1) * 128] * (1.0 / math.sqrt(8))
            q = both_halves(q, place % 2)
            for k in range(4):
                own = row // 8 == 2 * k + lane // 64
                q_out[e, :, k * 128:(k + 1) * 128] = jnp.where(own, q, 0.0).astype(BF)


def attend_kernel(all_ref, place_ref, qvg_ref, key_ref, wide_ref, left_ref, right_ref, used_ref,
                  scale_ref, absent_ref, out_ref, raw_ref, k_ref, q_ref, v_ref, gate_ref,
                  left_scr, right_scr):
    project(all_ref, qvg_ref, key_ref, raw_ref, k_ref, q_ref, v_ref, gate_ref)
    terms = [all_ref[peer, 4:12].astype(F32).reshape(64, 128).astype(BF) for peer in range(8)]
    bias = dot(jnp.concatenate(terms, axis=1), place_ref[...])
    bias = bias + jnp.concatenate([absent_ref[...]] * 4, axis=1)
    lane = iota((8, 128), 1)
    probs = []
    for e in range(8):
        keys = k_ref[e // 4, e % 4 * 64:(e % 4 + 1) * 64, :]
        scores = dot(keys, q_ref[e]) + bias
        expo = jnp.exp(scores - jnp.max(scores, axis=0, keepdims=True))
        probs.append((expo * (1.0 / jnp.sum(expo, axis=0, keepdims=True))).astype(BF))
    columns = []
    for pair in range(4):
        full = [dot(v_ref[2 * pair + odd], probs[2 * pair + odd]) for odd in range(2)]
        heads = []
        for h in range(8):
            low, high = [f[h * 8:(h + 1) * 8, h // 2 * 128:(h // 2 + 1) * 128] for f in full]
            if h % 2 == 0:
                high = pltpu.roll(high, 64, axis=1)
            else:
                low = pltpu.roll(low, 64, axis=1)
            heads.append(jnp.where(lane < 64, low, high))
        columns.append(jnp.concatenate(heads, axis=0))
    context = jnp.concatenate(columns, axis=1)
    gated = (gate_ref[...] * context).astype(BF)

    used = used_ref[...]
    wide = wide_ref[...]
    x = raw_ref[...] + dot_tn(wide[:, 0:64], gated).astype(BF).astype(F32) * used
    x = x - jnp.mean(x, axis=0, keepdims=True)
    x = (x * lax.rsqrt(jnp.mean(x * x, axis=0, keepdims=True) + 1e-05)).astype(BF)

    left = dot_tn(left_ref[...], x) * scale_ref[...]
    for e in range(8):
        both = left[:, e // 2 * 128:(e // 2 + 1) * 128]
        left_scr[e * 32:(e + 1) * 32, :] = both_halves(both, e % 2)
    for c in range(16):
        block = jnp.where(lane < 64, left_scr[pl.ds(2 * c, 8, stride=32), :],
                          left_scr[pl.ds(2 * c + 1, 8, stride=32), :]).astype(BF)
        for peer in range(8):
            out_ref[peer, c] = block

    update = dot_tn(gated, wide)
    for place in range(4):
        low, high = [e * 64 for e in (place, place + 4)]
        first = jnp.where(iota((64, 128), 1) < 64,
                          update[low:low + 64] * used[:, low:low + 1],
                          update[high:high + 64] * used[:, high:high + 1])
        first = first.reshape(8, 8, 128).astype(BF)
        for peer in range(8):
            out_ref[peer, 16 + place] = first[peer]

    right_scr[...] = dot_tn(x, right_ref[...])
    for peer in range(8):
        for quad in range(2):
            first = peer * 8 + quad * 4
            a, b, c, d = [right_scr[pl.ds(first + j, 8, stride=64), :] for j in range(4)]
            block = jnp.where(lane < 64, jnp.where(lane < 32, a, b), jnp.where(lane < 96, c, d))
            out_ref[peer, 20 + quad] = block.astype(BF)


def outer_kernel(keep_ref, all_ref, weight_ref, out_ref, outer_scr, part_scr):
    def gathered(block):
        return all_ref[:, block].astype(F32).reshape(64, 128)

    right = jnp.concatenate([gathered(20), gathered(21)], axis=1) * keep_ref[...]
    right = right.astype(BF)
    lane = iota((64, 128), 1)
    for m in range(8):
        left = [gathered(c).astype(BF) for c in (2 * m, 2 * m + 1)]
        outer = dot_tn(jnp.concatenate(left, axis=1), right)
        for quad in range(2):
            pieces = [outer[k * 64:(k + 1) * 64, quad * 128:(quad + 1) * 128] for k in range(4)]
            for j in range(4):
                turned = [pltpu.roll(p, (k - j) * 32 % 128, axis=1) if k != j else p
                          for k, p in enumerate(pieces)]
                low = jnp.where(lane < 32, turned[0], turned[1])
                high = jnp.where(lane < 96, turned[2], turned[3])
                row = (quad * 4 + j) * 64
                outer_scr[row:row + 64, m * 128:(m + 1) * 128] = (
                    jnp.where(lane < 64, low, high).astype(BF))
    part = dot(outer_scr[...], weight_ref[...])
    for j in range(8):
        part_scr[pl.ds(j, 64, stride=8), :] = part[j * 64:(j + 1) * 64]
    out_ref[...] = part_scr[...].reshape(64, 8, 128).astype(BF)


def finish_kernel(arrived_ref, all_ref, inverse_ref, shift_ref, update_out, pair_out):
    for place in range(4):
        block = all_ref[:, 16 + place].astype(F32)
        for half in range(2):
            part = block[:, :, half * 64:(half + 1) * 64].astype(BF)
            for peer in range(8):
                update_out[peer * 8 + half * 4 + place] = part[peer]
    total = jnp.sum(arrived_ref[...].astype(F32), axis=0)
    pair_out[0] = (total * inverse_ref[...] + shift_ref[...]).astype(BF)


def call(kernel, outs, specs, scratch=(), flops=0, limit=8):
    return pl.pallas_call(
        kernel,
        out_shape=[jax.ShapeDtypeStruct(shape, kind) for shape, kind in outs],
        in_specs=specs,
        out_specs=[VMEM] * len(outs),
        scratch_shapes=[s if not isinstance(s, tuple) else pltpu.VMEM(*s) for s in scratch],
        cost_estimate=pl.CostEstimate(flops=flops, bytes_accessed=1 << 20, transcendentals=0),
        compiler_params=pltpu.CompilerParams(vmem_limit_bytes=limit << 20),
    )


def local(
    alignment_rows,
    pair_features,
    sequence_block_count,
    cluster_member_count,
    residue_present_mask,
    attention_in_weight,
    attention_out_weight,
    pair_bias_weight,
    outer_factor_weight,
    outer_output_weight,
    outer_product_bias,
):
    members = cluster_member_count.reshape(1, 64)
    count = sequence_block_count.reshape(1, 1)
    (packed,) = call(
        pack_kernel, [((8, 4, 8, 128), BF)], [VMEM], flops=1 << 30,
    )(alignment_rows)
    (bias_send,) = call(
        bias_kernel, [((64, 1, 128), F32)], [HBM] * 4,
        [((8, 128), BF), ((8, 128), F32), ((1, 64), jnp.int32), pltpu.SMEM((1,), jnp.int32),
         pltpu.SemaphoreType.DMA((4,))],
        limit=60,
    )(pair_features.reshape(8, 128), pair_bias_weight.T, members, sequence_block_count)
    bias_all = lax.all_to_all(bias_send, "seq", split_axis=0, concat_axis=0, tiled=True)
    bias_all = bias_all.reshape(64, 128)
    tables = call(
        weight_kernel,
        [((1024, 128), BF), ((1024, 512), BF), ((2, 192, 128), BF), ((2, 128, 64), BF),
         ((64, 128), BF), ((64, 32), BF), ((64, 128), BF), ((8, 128), F32), ((1, 512), F32),
         ((1, 512), F32), ((64, 128), F32), ((1, 256), F32)],
        [VMEM] * 8, flops=1 << 30,
    )(outer_output_weight, attention_in_weight, attention_out_weight, outer_factor_weight,
      outer_product_bias.reshape(1, 128), members, residue_present_mask.reshape(1, 64), count)
    outer_w, place, qvg_w, key_w, wide_w, left_w, right_w, shift, used, scale, absent, keep = tables
    send, inverse = call(
        send_kernel, [((8, 12, 8, 128), BF), ((8, 128), F32)], [VMEM] * 3,
    )(packed, bias_all, keep)
    rows_all = lax.all_to_all(send, "res", split_axis=0, concat_axis=0, tiled=True)
    (factor_send,) = call(
        attend_kernel, [((8, 22, 8, 128), BF)], [VMEM] * 10,
        [((64, 512), F32), ((2, 256, 64), BF), ((8, 64, 512), BF), ((8, 64, 64), BF),
         ((64, 512), F32), ((256, 128), F32), ((512, 128), F32)],
    )(rows_all, place, qvg_w, key_w, wide_w, left_w, right_w, used, scale, absent)
    factor_all = lax.all_to_all(factor_send, "res", split_axis=0, concat_axis=0, tiled=True)
    (partial,) = call(
        outer_kernel, [((64, 8, 128), BF)], [VMEM] * 3, [((512, 1024), BF), ((512, 128), F32)],
    )(keep, factor_all, outer_w)
    arrived = lax.all_to_all(partial, "seq", split_axis=0, concat_axis=0, tiled=True)
    row_attention_update, pair_update = call(
        finish_kernel, [((64, 8, 64), BF), ((1, 8, 128), BF)], [VMEM] * 4,
    )(arrived, factor_all, inverse, shift)
    return (row_attention_update, pair_update)


def solution(mesh):
    return jax.shard_map(
        local,
        mesh=mesh,
        in_specs=(
            P("seq", "res", None),
            P("res", "seq", None),
            P("seq"),
            P("seq"),
            P(),
            P(),
            P(),
            P(),
            P(),
            P(),
            P(),
        ),
        out_specs=(P("seq", "res", None), P("seq", "res", None)),
        check_vma=False,
    )
```

time: 84.5 us -> 78.7 us (0.931)
  blocking collectives: 14 us -> 47 us
  waiting for transfers between devices: 25.2 us -> 6.74 us
  starting transfers between devices: 29.4 us -> 14.8 us
  Pallas kernels: 10.7 us -> 6.58 us
  other arithmetic: 1.85 us -> 0 us
    all_to_all x0 -> x2, blocking collectives: none -> 33 us  [the longest x1 17.4 us: local(): lax.all_to_all(partial, 'seq', split_axis=0, concat_axis=0, tiled=True)]
    all_to_all x2 -> x0, waiting for transfers between devices: 17 us -> none  [the longest x1 9.04 us: local(): lax.all_to_all(partial, 'seq', split_axis=0, concat_axis=0, tiled=True)]
    all_to_all x2 -> x0, starting transfers between devices: 14.6 us -> none  [the longest x1 7.74 us: local(): lax.all_to_all(partial, 'seq', split_axis=0, concat_axis=0, tiled=True)]
    pallas_call x5, Pallas kernels: 8.94 us -> 4.86 us  [the longest x1 2.18 us: local(): call(attend_kernel, [((8, 22, 8, 128), BF)], [VMEM] * 10, [((64, 512), F3...]
    all_to_all x1, waiting for transfers between devices: 8.23 us -> 6.74 us  [local(): lax.all_to_all(bias_send, 'seq', split_axis=0, concat_axis=0, tiled=True)]
    convert_element_type x1 -> x0, other arithmetic: 1.13 us -> none  [local(): pair_update = (summed / weight_sum + outer_product_bias).astype(BF)]
  transfers between devices with their start and end apart: 3 -> 1, of which waited for: 3 -> 1; matrix products, arithmetic and copies ran while one was open for 1% -> 0% of each run, Pallas kernels for 2% -> 1%
where the time goes in v5:
time: 78.7 us; the launch traced here: 78.4 us
  blocking collectives  47 us (60%)
  starting transfers between devices  14.8 us (19%)
  waiting for transfers between devices  6.74 us (9%)
  Pallas kernels  6.58 us (8%)
  local copies, waits for them, and re-layouts  1.83 us (2%)
  between operations  1.38 us (2%)
    all_to_all x1, blocking collectives, local(): lax.all_to_all(partial, 'seq', split_axis=0, concat_axis=0, tiled=True)  17.4 us
    all_to_all x1, blocking collectives, local(): lax.all_to_all(send, 'res', split_axis=0, concat_axis=0, tiled=True)  15.6 us
    all_to_all x1, starting transfers between devices, local(): lax.all_to_all(bias_send, 'seq', split_axis=0, concat_axis=0, tiled=True)  14.8 us
    all_to_all x1, blocking collectives, local(): lax.all_to_all(factor_send, 'res', split_axis=0, concat_axis=0, tiled=True)  14 us
    all_to_all x1, waiting for transfers between devices, local(): lax.all_to_all(bias_send, 'seq', split_axis=0, concat_axis=0, tiled=True)  6.74 us
    pallas_call x1, Pallas kernels, local(): call(attend_kernel, [((8, 22, 8, 128), BF)], [VMEM] * 10, [((64, 512), F3...  2.18 us
    unnamed x16, local copies, waits for them, and re-layouts  1.83 us
    pallas_call x1, Pallas kernels, local(): call(bias_kernel, [((64, 1, 128), F32)], [HBM] * 4, [((8, 128), BF), ((8,...  1.64 us
  transfers between devices with their start and end apart: 1, of which 1 were waited for; matrix products, arithmetic and copies ran while one was open for 0% of the time, Pallas kernels for 1%

profile of v5, /device:TPU:1, one launch (start us, length us, event | category | flops | bytes accessed | tf_op | source)
XLA Modules:
  0.0 78.4 jit_solution(7073239943406789839)
XLA Ops:
  1.3 1.6 %shard_map.124 = f32[64,1,128]{2,1,0:T(1,128)} custom-call(bf16[8,128]{1,0:T(8,128)(2,1)} %bitcast.14, f32[8,128]{1,0:T(8,128)} %bitcast.13, s32[1,64]{1,0:T(1,128)} %bitcast.9, s32[1]{0:T(128)} %copy.14.count_hbm), custom_call_target="tpu_custom_call" | custom-call | bytes 1048576 | tf_op jit(solution)/shard_map/pallas_call | solution.py:290
  2.9 14.8 %all-to-all-start = ((f32[64,1,128]{2,1,0:T(1,128)}), f32[64,1,128]{2,1,0:T(1,128)S(1)}, u32[]{:S(2)}, u32[]{:S(2)}) async-start(f32[64,1,128]{2,1,0:T(1,128)} %shard_map.124), calls=%async_computation | async-start | bytes 65536 | tf_op jit(solution)/shard_map/all_to_all | solution.py:296
  17.8 0.0 copy-start.2
  17.8 0.9 %copy-done.2 = bf16[64,8,64]{2,1,0:T(8,128)(2,1)S(1)} copy-done((bf16[64,8,64]{2,1,0:T(8,128)(2,1)S(1)}, bf16[64,8,64]{2,1,0:T(8,128)(2,1)}, u32[]{:S(2)}) %copy-start.2) | copy-done | bytes 65560
  18.7 0.0 copy-start.1
  18.7 0.0 copy-start.3
  18.7 0.0 copy-start.4
  18.7 0.0 copy-start.5
  18.7 0.1 shard_map.123.rows_ref
  18.8 0.0 copy-start
  18.8 0.0 copy-start.6
  18.8 0.0 copy-start.7
  18.8 0.9 %copy-done.1 = f32[1024,128]{1,0:T(8,128)S(1)} copy-done((f32[1024,128]{1,0:T(8,128)S(1)}, f32[1024,128]{1,0:T(8,128)}, u32[]{:S(2)}) %copy-start.1) | copy-done | bytes 524312
  19.7 0.0 copy-done.3
  19.7 0.0 copy-done.4
  19.7 0.0 copy-done.5
  19.7 0.0 copy-done
  19.7 0.0 copy-done.6
  19.7 0.0 copy-done.7
  19.7 0.5 shard_map.122
  20.3 6.7 %all-to-all-done = f32[64,1,128]{2,1,0:T(1,128)S(1)} async-done(((f32[64,1,128]{2,1,0:T(1,128)}), f32[64,1,128]{2,1,0:T(1,128)S(1)}, u32[]{:S(2)}, u32[]{:S(2)}) %all-to-all-start) | async-done | bytes 32800 | tf_op jit(solution)/shard_map/all_to_all | solution.py:296
  27.0 0.1 shard_map.125
  27.1 15.6 %all_to_all.20.all_ref = bf16[8,12,8,128]{3,2,1,0:T(8,128)(2,1)S(1)} all-to-all(bf16[8,12,8,128]{3,2,1,0:T(8,128)(2,1)S(1)} %get-tuple-element.17), channel_id=1, replica_groups=mesh['seq'=64,'res'=8] {'res'}, dimensions={0} | all-to-all | bytes 393216 | tf_op jit(solution)/shard_map/all_to_all | solution.py:310
  42.7 2.2 %shard_map.126 = bf16[8,22,8,128]{3,2,1,0:T(8,128)(2,1)S(1)} custom-call(bf16[8,12,8,128]{3,2,1,0:T(8,128)(2,1)S(1)} %all_to_all.20.all_ref, bf16[1024,512]{1,0:T(8,128)(2,1)S(1)} %get-tuple-element.18.place_ref, bf16[2,192,128]{2,1,0:T(8,128)(2,1)S(1)} %get-tuple-element.19.qvg_ref, bf16[2,128,64]{2,1,0:T(8,128)(2,1)S(1)} %get-tuple-element.20.key_ref, ...), custom_call_target="tpu_custom_call" | custom-call | bytes 1048576 | tf_op jit(solution)/shard_map/pallas_call | solution.py:311
  44.9 14.0 %all_to_all.21.all_ref = bf16[8,22,8,128]{3,2,1,0:T(8,128)(2,1)S(1)} all-to-all(bf16[8,22,8,128]{3,2,1,0:T(8,128)(2,1)S(1)} %shard_map.126), channel_id=1, replica_groups=mesh['seq'=64,'res'=8] {'res'}, dimensions={0} | all-to-all | bytes 720896 | tf_op jit(solution)/shard_map/all_to_all | solution.py:316
  58.9 1.3 %shard_map.127 = bf16[64,8,128]{2,1,0:T(8,128)(2,1)S(1)} custom-call(f32[1,256]{1,0:T(1,128)S(1)} %get-tuple-element.16.ahead_ref.keep_ref, bf16[8,22,8,128]{3,2,1,0:T(8,128)(2,1)S(1)} %all_to_all.21.all_ref, bf16[1024,128]{1,0:T(8,128)(2,1)S(1)} %get-tuple-element.27.weight_ref), custom_call_target="tpu_custom_call" | custom-call | bytes 1048576 | tf_op jit(solution)/shard_map/pallas_call | solution.py:317
  60.2 17.4 %all_to_all.22.arrived_ref = bf16[64,8,128]{2,1,0:T(8,128)(2,1)S(1)} all-to-all(bf16[64,8,128]{2,1,0:T(8,128)(2,1)S(1)} %shard_map.127), channel_id=1, replica_groups=mesh['seq'=64,'res'=8] {'seq'}, dimensions={0} | all-to-all | bytes 262144 | tf_op jit(solution)/shard_map/all_to_all | solution.py:320
  77.6 0.8 shard_map.128
Async XLA Ops:
  2.9 24.1 %all-to-all-start = ((f32[64,1,128]{2,1,0:T(1,128)}), f32[64,1,128]{2,1,0:T(1,128)S(1)}, u32[]{:S(2)}, u32[]{:S(2)}) async-start(f32[64,1,128]{2,1,0:T(1,128)} %shard_map.124), calls=%async_computation | async-start | bytes 65536 | tf_op jit(solution)/shard_map/all_to_all | solution.py:296
  17.8 0.9 %copy-start.2 = (bf16[64,8,64]{2,1,0:T(8,128)(2,1)S(1)}, bf16[64,8,64]{2,1,0:T(8,128)(2,1)}, u32[]{:S(2)}) copy-start(bf16[64,8,64]{2,1,0:T(8,128)(2,1)} %rows_ref.1) | copy-start | bytes 196612
  18.7 1.0 %copy-start.1 = (f32[1024,128]{1,0:T(8,128)S(1)}, f32[1024,128]{1,0:T(8,128)}, u32[]{:S(2)}) copy-start(f32[1024,128]{1,0:T(8,128)} %outer_w_ref.1) | copy-start | bytes 1572868
  18.7 1.0 %copy-start.3 = (bf16[64,256]{1,0:T(8,128)(2,1)S(1)}, bf16[64,256]{1,0:T(8,128)(2,1)}, u32[]{:S(2)}) copy-start(bf16[64,256]{1,0:T(8,128)(2,1)} %in_w_ref.1) | copy-start | bytes 98308
  18.7 1.0 %copy-start.4 = (bf16[64,64]{1,0:T(8,128)(2,1)S(1)}, bf16[64,64]{1,0:T(8,128)(2,1)}, u32[]{:S(2)}) copy-start(bf16[64,64]{1,0:T(8,128)(2,1)} %out_w_ref.1) | copy-start | bytes 24580
  18.7 1.0 %copy-start.5 = (bf16[64,64]{1,0:T(8,128)(2,1)S(1)}, bf16[64,64]{1,0:T(8,128)(2,1)}, u32[]{:S(2)}) copy-start(bf16[64,64]{1,0:T(8,128)(2,1)} %factor_ref.1) | copy-start | bytes 24580
  18.8 0.9 %copy-start = (s32[64]{0:T(128)S(1)}, s32[64]{0:T(128)}, u32[]{:S(2)}) copy-start(s32[64]{0:T(128)} %param.14) | copy-start | bytes 772
  18.8 0.9 %copy-start.6 = (f32[128]{0:T(128)S(1)}, f32[128]{0:T(128)}, u32[]{:S(2)}) copy-start(f32[128]{0:T(128)} %param.21) | copy-start | bytes 1540
  18.8 0.9 %copy-start.7 = (s32[64]{0:T(128)S(1)}, s32[64]{0:T(128)}, u32[]{:S(2)}) copy-start(s32[64]{0:T(128)} %param.15) | copy-start | bytes 772
